TPU v7x, 128 devices: a whole 4x4x4 slice. The times are simulated.
128 devices in a mesh: sub: 32 (over x, z, core), grp: 4 (over y).
Axes of the slice: x: 4, y: 4, z: 4, core: 2. Of those that a mesh axis runs over, the one named last changes fastest.
Arguments:
- solution: float32 [128, 128, 2048], P(('sub', 'grp')), may hold values from -6 to 6
- residual: float32 [128, 128, 2048], P(('sub', 'grp'))
- direction: float32 [128, 128, 2048], P(('sub', 'grp'))
- residual_product: float32 [128], replicated, may hold values from 262144 to 5242880
- neighbor_slots: int32 [128, 4], P(('sub', 'grp')), may hold values from 0 to 3, each once within a row
- coupling: bfloat16 [128, 96, 256, 128], P(('sub', 'grp')), may hold values from -0.375 to 0.375
- dirichlet_factor: bfloat16 [128, 96, 128, 128], P(('sub', 'grp')), may hold values from -0.5 to 0.5
- face_block: bfloat16 [128, 32, 128, 128], P(('sub', 'grp')), as said below
- neumann_factor: bfloat16 [128, 32, 128, 128], P(('sub', 'grp')), may hold values from -0.5 to 0.5
- primal_block: int32 [128, 128], P(('sub', 'grp')), may hold values from 0 to 31
- primal_basis: bfloat16 [128, 128, 128], P(('sub', 'grp')), may hold values from -1.5 to 1.5
- coarse_matrix: float32 [128, 9, 128, 128], P(('sub', 'grp')), may hold values from -0.17677669 to 0.17677669
- coarse_block_inverse: float32 [128, 128, 128], P(('sub', 'grp')), may hold values from -0.5 to 0.5
- coarse_pattern: int32 [128, 9], P(('sub', 'grp')), may hold values from 0 to 127, as said below
Outputs:
- new_solution: float32 [128, 128, 2048], P(('sub', 'grp'))
- new_residual: float32 [128, 128, 2048], P(('sub', 'grp'))
- new_direction: float32 [128, 128, 2048], P(('sub', 'grp'))
- new_product: float32 [128], replicated
Inputs may be any that keep to these rules, and one draw needn't show every extreme that they name: `neighbor_slots`: each row orders the four local face slots: entry d is the slot of the face toward direction d (sub lower, sub upper, grp lower, grp upper). `coarse_pattern`: row t names 9 different subdomains, the first of them t itself; subdomain s lies on the device of index s along sub+grp, and every entry lies within 2 positions of row t along sub, cyclically. `face_block`: each block is symmetric with every eigenvalue at least 0.5.
All inputs are finite; a program needn't handle non-finite values.
Results may differ from a plain program's by a relative error of at most 0.0003.
Values sent between devices are 32-bit elements; how exact they have to be, the bound alone decides.
A program may use at most 128 MiB of HBM per device.

v0:
```python
import functools

import jax
import jax.numpy as jnp
from jax import lax
from jax.sharding import Mesh
from jax.sharding import PartitionSpec as P

REACH_SUBS = 2
SUB = ("sub_0", "sub_1", "sub_2")
SUB_GRP = ("sub_0", "sub_1", "sub_2", "grp")


highest_precision = lax.Precision.HIGHEST


def shifted(value, axis, steps):
    count = lax.axis_size(axis)
    pairs = [(source, (source + steps) % count) for source in range(count)]
    return lax.ppermute(value, axis, pairs)


def joined_along(pieces, dim):
    dims = list(pieces.shape[1:])
    dims[dim] *= pieces.shape[0]
    return jnp.moveaxis(pieces, 0, dim).reshape(dims)


def from_everyone(array, axis):
    copies = jnp.broadcast_to(array, (lax.axis_size(axis), *array.shape))
    return lax.all_to_all(copies, axis, split_axis=0, concat_axis=0, tiled=True)


def collect_2(array, axis, dim):
    return joined_along(from_everyone(array, axis), dim)


def by_axis(array, axes):
    return functools.reduce(lax.psum, axes, array)


def slot_table(neighbor_slots):
    return (neighbor_slots[0][:, None] == jnp.arange(4, dtype=jnp.int32)[None, :]).astype(
        jnp.float32
    )


def place_faces(directed, slot_onehot, block_width):
    load_count = directed.shape[1]
    face_width = directed.shape[2]
    placed = jnp.einsum("dk,dlf->lkf", slot_onehot, directed, precision=highest_precision)
    return placed.reshape(load_count, 4 * face_width // block_width, block_width)


def spread(owned_part, slot_onehot, block_width):
    face_width = owned_part.shape[2] // 2
    own_sub = owned_part[:, :, :face_width]
    own_grp = owned_part[:, :, face_width:]
    from_sub = shifted(own_sub, SUB, 1)
    from_grp = shifted(own_grp, "grp", 1)
    directed = jnp.stack([from_sub[0], own_sub[0], from_grp[0], own_grp[0]], 0)
    return place_faces(directed, slot_onehot, block_width)


def collect(local_part, slot_onehot):
    load_count = local_part.shape[0]
    placed = local_part.reshape(load_count, 4, -1)
    directed = jnp.einsum("dk,lkf->dlf", slot_onehot, placed, precision=highest_precision)
    to_sub = shifted(directed[0][None], SUB, -1)
    to_grp = shifted(directed[2][None], "grp", -1)
    owned_sub = directed[1][None] + to_sub
    owned_grp = directed[3][None] + to_grp
    return jnp.concatenate([owned_sub, owned_grp], 2)


def condensed(vector, couple, dirichlet, face_matrix):
    count_of_blocks = vector.shape[1]
    block_width = vector.shape[2]
    paired = jnp.concatenate(
        [
            jnp.concatenate([vector, jnp.roll(vector, -(offset + 1), axis=1)], 2)
            for offset in range(3)
        ],
        1,
    )
    interior = jnp.einsum("lib,ibk->lik", paired, couple, precision=highest_precision)
    middle = jnp.einsum("lik,ikm->lim", interior, dirichlet, precision=highest_precision)
    solved = jnp.einsum("lim,ikm->lik", middle, dirichlet, precision=highest_precision)
    returned = jnp.einsum("lik,ibk->lib", solved, couple, precision=highest_precision)
    result = jnp.einsum("ljb,jbk->ljk", vector, face_matrix, precision=highest_precision)
    for offset in range(3):
        portion = returned[:, offset * count_of_blocks : (offset + 1) * count_of_blocks]
        result = (
            result
            + portion[:, :, :block_width]
            + jnp.roll(portion[:, :, block_width:], offset + 1, axis=1)
        )
    return result


def coarse_neighbors(initial_step, pattern, matrix):
    load_count, primal_count = initial_step.shape
    grp_count = lax.axis_size("grp")
    sub_count = lax.axis_size(SUB)
    reach_count = 2 * REACH_SUBS + 1
    entry_sub = pattern // grp_count
    entry_grp = pattern % grp_count
    position = (entry_sub - lax.axis_index(SUB) + REACH_SUBS) % sub_count
    column = collect_2(initial_step[None], "grp", 0)
    pieces = []
    for place in range(reach_count):
        if place == REACH_SUBS:
            pieces.append(column)
        else:
            pieces.append(shifted(column, SUB, REACH_SUBS - place))
    window = jnp.stack(pieces, 0).reshape(-1, load_count, primal_count)
    slot_index = position * grp_count + entry_grp
    chooser = (slot_index[:, None] == jnp.arange(window.shape[0], dtype=jnp.int32)[None, :]).astype(
        jnp.float32
    )
    chosen = jnp.einsum("kj,jlc->klc", chooser, window, precision=highest_precision)
    return jnp.einsum("klc,kcd->ld", chosen, matrix, precision=highest_precision)


def precondition(
    local_copy, slot_onehot, neumann, block_ids, primal_rows, matrix, inverse, pattern
):
    halved = local_copy * 0.5
    neumann_step = jnp.einsum("ljb,jbk->ljk", halved, neumann, precision=highest_precision)
    local_solve = jnp.einsum("ljk,jmk->ljm", neumann_step, neumann, precision=highest_precision)
    selector = (block_ids[:, None] == jnp.arange(halved.shape[1], dtype=jnp.int32)[None, :]).astype(
        jnp.float32
    )
    picked = jnp.einsum("ljb,cj->lcb", halved, selector, precision=highest_precision)
    coarse_residual = jnp.einsum("lcb,cb->lc", picked, primal_rows, precision=highest_precision)
    initial_step = jnp.dot(coarse_residual, inverse, precision=highest_precision)
    adjacent_sum = coarse_neighbors(initial_step, pattern, matrix)
    coarse_correction = initial_step + jnp.dot(
        coarse_residual - adjacent_sum, inverse, precision=highest_precision
    )
    weighted = coarse_correction[:, :, None] * primal_rows[None]
    spread_back = jnp.einsum("lcb,cj->ljb", weighted, selector, precision=highest_precision)
    return collect(0.5 * (local_solve + spread_back), slot_onehot)


def shards(
    solution,
    residual,
    direction,
    residual_product,
    neighbor_slots,
    coupling,
    dirichlet_factor,
    face_block,
    neumann_factor,
    primal_block,
    primal_basis,
    coarse_matrix,
    coarse_block_inverse,
    coarse_pattern,
):
    slot_onehot = slot_table(neighbor_slots)
    block_width = face_block.shape[2]
    couple = coupling[0].astype(jnp.float32)
    dirichlet = dirichlet_factor[0].astype(jnp.float32)
    face_matrix = face_block[0].astype(jnp.float32)
    neumann = neumann_factor[0].astype(jnp.float32)
    primal_rows = primal_basis[0].astype(jnp.float32)
    direction_local = spread(direction, slot_onehot, block_width)
    image = collect(condensed(direction_local, couple, dirichlet, face_matrix), slot_onehot)
    curvature = by_axis(jnp.sum(direction * image, axis=(0, 2)), SUB_GRP)
    step_length = residual_product / curvature
    new_residual = residual - step_length[None, :, None] * image
    new_local = spread(new_residual, slot_onehot, block_width)
    preconditioned = precondition(
        new_local,
        slot_onehot,
        neumann,
        primal_block[0],
        primal_rows,
        coarse_matrix[0],
        coarse_block_inverse[0],
        coarse_pattern[0],
    )
    new_product = by_axis(jnp.sum(new_residual * preconditioned, axis=(0, 2)), SUB_GRP)
    new_solution = solution + step_length[None, :, None] * direction
    step_ratio = new_product / residual_product
    new_direction = preconditioned + step_ratio[None, :, None] * direction
    return (new_solution, new_residual, new_direction, new_product)


def solution(mesh):
    split = Mesh(
        mesh.devices.reshape(4, 4, 2, mesh.shape["grp"]), ("sub_0", "sub_1", "sub_2", "grp")
    )
    return jax.shard_map(
        shards,
        mesh=split,
        in_specs=(
            P(SUB_GRP, None, None),
            P(SUB_GRP, None, None),
            P(SUB_GRP, None, None),
            P(),
            P(SUB_GRP, None),
            P(SUB_GRP, None, None, None),
            P(SUB_GRP, None, None, None),
            P(SUB_GRP, None, None, None),
            P(SUB_GRP, None, None, None),
            P(SUB_GRP, None),
            P(SUB_GRP, None, None),
            P(SUB_GRP, None, None, None),
            P(SUB_GRP, None, None),
            P(SUB_GRP, None),
        ),
        out_specs=(P(SUB_GRP, None, None), P(SUB_GRP, None, None), P(SUB_GRP, None, None), P()),
        check_vma=False,
    )
```

profile of v0, /device:TPU:0, one launch (start us, length us, event | category | flops | bytes accessed | tf_op | source)
XLA Modules:
  0.0 296.0 jit_solution(5695722564196463726)
XLA Ops:
  5.0 10.3 %collective-permute-done = f32[1,128,1024]{2,0,1:T(1,128)S(1)} collective-permute-done((f32[1,128,1024]{2,0,1:T(1,128)S(1)}, f32[1,128,1024]{2,0,1:T(1,128)S(1)}, u32[]{:S(2)}, u32[]{:S(2)}) %collective-permute-start) | collective-permute-done | bytes 524320 | tf_op jit(solution)/shard_map/ppermute | solution.py:20
  18.1 5.2 %fusion.45 = f32[128,4,1024]{2,1,0:T(4,128)} fusion(f32[1,128,1024]{2,0,1:T(1,128)S(1)} %copy.71, f32[1,128,1024]{2,0,1:T(1,128)S(1)} %collective-permute-done.1, f32[1,128,1024]{2,0,1:T(1,128)S(1)} %copy.70, f32[1,128,1024]{2,0,1:T(1,128)S(1)} %collective-permute-done, s32[4]{0:T(128)S(1)} %bitcast.127), kind=kOutput, calls=%fused_computation.46 | convolution fusion | flops 26738704 | bytes 4194320 | tf_op jit(solution)/shard_map/dk,dlf->lkf/dot_general | solution.py:51
  29.4 5.8 %maximum_maximum_fusion = f32[128,96,256]{2,1,0:T(8,128)} fusion(f32[128,3,128]{2,1,0:T(4,128)S(1)} %slice.143, f32[128,29,128]{2,1,0:T(8,128)S(1)} %slice.142, f32[128,32,128]{2,1,0:T(8,128)S(1)} %copy-done.2, f32[128,2,128]{2,1,0:T(2,128)S(1)} %slice.141, f32[128,30,128]{2,1,0:T(8,128)S(1)} %slice.140, f32[128,1,128]{2,1,0:T(1,128)S(1)} %slice.139, ...), kind=kLoop, calls=%fused_computation | loop fusion | flops 25165824 | bytes 20971520 | tf_op jit(solution)/shard_map/concatenate | solution.py:79
  35.2 21.7 %fusion = f32[96,128,128]{2,1,0:T(8,128)} fusion(f32[128,96,256]{2,1,0:T(8,128)} %maximum_maximum_fusion, bf16[1,96,256,128]{3,2,1,0:T(8,128)(2,1)} %param.19), kind=kOutput, calls=%fused_computation.1 | convolution fusion | flops 4831838208 | bytes 25165824 | tf_op jit(solution)/shard_map/lib,ibk->lik/dot_general | solution.py:86
  56.9 5.3 %fusion.11 = f32[96,128,128]{2,1,0:T(8,128)S(1)} fusion(f32[96,128,128]{2,1,0:T(8,128)} %fusion, bf16[1,96,128,128]{3,2,1,0:T(8,128)(2,1)S(1)} %copy-done), kind=kOutput, calls=%fused_computation.12 | convolution fusion | flops 2415919104 | bytes 15728640 | tf_op jit(solution)/shard_map/lik,ikm->lim/dot_general | solution.py:87
  62.2 8.5 %fusion.9 = f32[96,128,128]{2,1,0:T(8,128)} fusion(f32[96,128,128]{2,1,0:T(8,128)S(1)} %fusion.11, bf16[1,96,128,128]{3,2,1,0:T(8,128)(2,1)S(1)} %copy-done), kind=kOutput, calls=%fused_computation.10 | convolution fusion | flops 2415919104 | bytes 15728640 | tf_op jit(solution)/shard_map/lim,ikm->lik/dot_general | solution.py:88
  70.7 8.4 %fusion.15 = f32[128,96,256]{0,2,1:T(8,128)S(1)} fusion(bf16[1,96,256,128]{3,2,1,0:T(8,128)(2,1)} %param.19, f32[96,128,128]{2,1,0:T(8,128)} %fusion.9), kind=kOutput, calls=%fused_computation.16 | convolution fusion | flops 4831838208 | bytes 25165824 | tf_op jit(solution)/shard_map/lik,ibk->lib/dot_general | solution.py:89
  81.4 5.5 %fusion.24 = f32[128,32,128]{0,2,1:T(8,128)} fusion(f32[128,96,256]{0,2,1:T(8,128)S(1)} %fusion.15, f32[128,31,128]{0,2,1:T(8,128)S(1)} %slice.146, f32[128,1,128]{0,2,1:T(8,128)S(1)} %slice.145, f32[128,30,128]{0,2,1:T(8,128)S(1)} %slice.149, f32[128,2,128]{0,2,1:T(8,128)S(1)} %slice.148, f32[128,29,128]{0,2,1:T(8,128)S(1)} %slice.152, ...), kind=kOutput, calls=%fused_computation.22 | convolution fusion | flops 810024960 | bytes 17825792 | tf_op jit(solution)/shard_map/ljb,jbk->ljk/dot_general | solution.py:90
  86.9 3.5 %copy.44 = f32[128,4,1024]{2,1,0:T(4,128)} copy(f32[128,4,1024]{0,2,1:T(8,128)} %bitcast.118) | data formatting | bytes 4194304 | tf_op jit(solution)/shard_map/reshape | solution.py:67
  90.3 3.7 %fusion.82 = f32[4,128,1024]{2,0,1:T(4,128)S(1)} fusion(f32[128,4,1024]{2,1,0:T(4,128)} %copy.44, s32[4]{0:T(128)S(1)} %bitcast.128), kind=kOutput, calls=%fused_computation.102 | convolution fusion | flops 25165840 | bytes 4194320 | tf_op jit(solution)/shard_map/dk,lkf->dlf/dot_general | solution.py:68
  95.7 5.2 %collective-permute-start.2 = (f32[1,128,1024]{2,1,0:T(8,128)S(1)}, f32[1,128,1024]{2,1,0:T(8,128)S(1)}, u32[]{:S(2)}, u32[]{:S(2)}) collective-permute-start(f32[1,128,1024]{2,1,0:T(8,128)S(1)} %copy.73), channel_id=1, source_target_pairs={{0,124},{4,0},{8,4},{12,8},{16,12},{20,16},{24,20},{28,24},{32,28}... | collective-permute-start | bytes 1572872 | tf_op jit(solution)/shard_map/ppermute | solution.py:20
  102.7 4.9 %collective-permute-done.2 = f32[1,128,1024]{2,1,0:T(8,128)S(1)} collective-permute-done((f32[1,128,1024]{2,1,0:T(8,128)S(1)}, f32[1,128,1024]{2,1,0:T(8,128)S(1)}, u32[]{:S(2)}, u32[]{:S(2)}) %collective-permute-start.2) | collective-permute-done | bytes 524320 | tf_op jit(solution)/shard_map/ppermute | solution.py:20
  111.1 10.6 %psum.56 = f32[128]{0:T(128)S(1)} all-reduce(f32[128]{0:T(128)S(1)} %multiply_reduce_fusion.1), channel_id=1, replica_groups=mesh['sub_0'=4,'sub_1'=4,'sub_2'=2,'grp'=4] {'sub_0'}, use_global_device_ids=true, to_apply=%region_1.2 | all-reduce | flops 128 | bytes 1024 | tf_op jit(solution)/shard_map/psum | solution.py:39
  121.7 11.3 %psum.57 = f32[128]{0:T(128)S(1)} all-reduce(f32[128]{0:T(128)S(1)} %psum.56), channel_id=1, replica_groups=mesh['sub_0'=4,'sub_1'=4,'sub_2'=2,'grp'=4] {'sub_1'}, use_global_device_ids=true, to_apply=%region_2.3 | all-reduce | flops 128 | bytes 1024 | tf_op jit(solution)/shard_map/psum | solution.py:39
  135.5 10.6 %psum.59 = f32[128]{0:T(128)S(1)} all-reduce(f32[128]{0:T(128)S(1)} %psum.58), channel_id=1, replica_groups=mesh['sub_0'=4,'sub_1'=4,'sub_2'=2,'grp'=4] {'grp'}, use_global_device_ids=true, to_apply=%region_4.5 | all-reduce | flops 128 | bytes 1024 | tf_op jit(solution)/shard_map/psum | solution.py:39
  148.9 10.9 %collective-permute-done.4 = f32[1,128,1024]{2,1,0:T(8,128)S(1)} collective-permute-done((f32[1,128,1024]{2,1,0:T(8,128)S(1)}, f32[1,128,1024]{2,1,0:T(8,128)S(1)}, u32[]{:S(2)}, u32[]{:S(2)}) %collective-permute-start.4) | collective-permute-done | bytes 524320 | tf_op jit(solution)/shard_map/ppermute | solution.py:20
  164.5 4.8 %multiply_bitcast_fusion = f32[128,4,1024]{2,1,0:T(4,128)} fusion(f32[4,128,1024]{2,1,0:T(8,128)S(1)} %pad_maximum_fusion, s32[4]{0:T(128)S(1)} %bitcast.129), kind=kOutput, calls=%fused_computation.45 | convolution fusion | flops 25690128 | bytes 4194320 | tf_op jit(solution)/shard_map/dk,dlf->lkf/dot_general | solution.py:51
  171.5 3.5 %fusion.66 = f32[128,128,128]{2,0,1:T(8,128)S(1)} fusion(f32[128,32,128]{2,1,0:T(8,128)S(1)} %mul.86, s32[128]{0:T(128)S(1)} %bitcast.131), kind=kOutput, calls=%fused_computation.80 | convolution fusion | flops 805310464 | bytes 10486272 | tf_op jit(solution)/shard_map/ljb,cj->lcb/dot_general | solution.py:134
  175.1 11.0 %fusion.2 = f32[128,1,128]{2,1,0:T(1,128)S(1)} fusion(f32[128,128,128]{2,0,1:T(8,128)S(1)} %fusion.66, bf16[128,128,1]{1,0,2:T(8,128)(2,1)S(1)} %bitcast.126), kind=kOutput, calls=%fused_computation.3 | convolution fusion | flops 25165824 | bytes 8486912 | tf_op jit(solution)/shard_map/lcb,cb->lc/dot_general | solution.py:135
  191.2 6.0 %all-to-all-done = f32[4,1,128,128]{3,2,1,0:T(8,128)S(1)} async-done(((f32[4,1,128,128]{3,2,1,0:T(8,128)}), f32[4,1,128,128]{3,2,1,0:T(8,128)S(1)}, u32[]{:S(2)}, u32[]{:S(2)}) %all-to-all-start) | async-done | bytes 262176 | tf_op jit(solution)/shard_map/all_to_all | solution.py:31
  198.4 4.8 %fusion.37 = f32[32,128,128]{2,1,0:T(8,128)} fusion(f32[128,32,128]{2,1,0:T(8,128)S(1)} %mul.86, bf16[1,32,128,128]{3,2,1,0:T(8,128)(2,1)} %param.22), kind=kOutput, calls=%fused_computation.38 | convolution fusion | flops 805306368 | bytes 5242880 | tf_op jit(solution)/shard_map/ljb,jbk->ljk/dot_general | solution.py:129
  203.2 5.1 %collective-permute-start.8 = (f32[4,128,128]{2,1,0:T(8,128)S(1)}, f32[4,128,128]{2,1,0:T(8,128)S(1)}, u32[]{:S(2)}, u32[]{:S(2)}) collective-permute-start(f32[4,128,128]{2,1,0:T(8,128)S(1)} %bitcast.122), channel_id=1, source_target_pairs={{0,124},{4,0},{8,4},{12,8},{16,12},{20,16},{24,20},{28,24},{32,28}... | collective-permute-start | bytes 786440 | tf_op jit(solution)/shard_map/ppermute | solution.py:20
  209.7 4.7 %collective-permute-done.8 = f32[4,128,128]{2,1,0:T(8,128)S(1)} collective-permute-done((f32[4,128,128]{2,1,0:T(8,128)S(1)}, f32[4,128,128]{2,1,0:T(8,128)S(1)}, u32[]{:S(2)}, u32[]{:S(2)}) %collective-permute-start.8) | collective-permute-done | bytes 262176 | tf_op jit(solution)/shard_map/ppermute | solution.py:20
  220.1 5.4 %fusion.5 = f32[32,128,128]{2,0,1:T(8,128)} fusion(f32[128,128]{1,0:T(8,128)S(1)} %copy-done.17, f32[128,128]{1,0:T(8,128)S(1)} %convolution_add_fusion, s32[128]{0:T(128)S(1)} %bitcast.132), kind=kOutput, calls=%fused_computation.6 | convolution fusion | flops 807407616 | bytes 2228736 | tf_op jit(solution)/shard_map/lcb,cj->ljb/dot_general | solution.py:142
  228.7 5.5 %add_multiply_fusion = f32[32,128,128]{1,2,0:T(8,128)} fusion(f32[32,128,128]{1,2,0:T(8,128)} %copy.51, f32[32,128,128]{2,1,0:T(8,128)S(1)} %copy-done.6, bf16[1,32,128,128]{3,2,1,0:T(8,128)(2,1)} %param.22), kind=kOutput, calls=%fused_computation.44 | convolution fusion | flops 806354944 | bytes 7340032 | tf_op jit(solution)/shard_map/ljk,jmk->ljm/dot_general | solution.py:130
  237.3 3.7 %fusion.80 = f32[4,128,1024]{2,0,1:T(4,128)S(1)} fusion(f32[128,4,1024]{2,1,0:T(4,128)} %copy.52, s32[4]{0:T(128)S(1)} %bitcast.130), kind=kOutput, calls=%fused_computation.101 | convolution fusion | flops 25165840 | bytes 4194320 | tf_op jit(solution)/shard_map/dk,lkf->dlf/dot_general | solution.py:68
  246.5 5.4 %collective-permute-done.10 = f32[1,128,1024]{2,1,0:T(8,128)S(1)} collective-permute-done((f32[1,128,1024]{2,1,0:T(8,128)S(1)}, f32[1,128,1024]{2,1,0:T(8,128)S(1)}, u32[]{:S(2)}, u32[]{:S(2)}) %collective-permute-start.10) | collective-permute-done | bytes 524320 | tf_op jit(solution)/shard_map/ppermute | solution.py:20
  252.0 5.2 %collective-permute-done.11 = f32[1,128,1024]{2,1,0:T(8,128)S(1)} collective-permute-done((f32[1,128,1024]{2,1,0:T(8,128)S(1)}, f32[1,128,1024]{2,1,0:T(8,128)S(1)}, u32[]{:S(2)}, u32[]{:S(2)}) %collective-permute-start.11) | collective-permute-done | bytes 524320 | tf_op jit(solution)/shard_map/ppermute | solution.py:20
  257.6 7.7 %psum.60 = f32[128]{0:T(128)S(1)} all-reduce(f32[128]{0:T(128)S(1)} %multiply_reduce_fusion), channel_id=1, replica_groups=mesh['sub_0'=4,'sub_1'=4,'sub_2'=2,'grp'=4] {'sub_0'}, use_global_device_ids=true, to_apply=%region_6.7 | all-reduce | flops 128 | bytes 1024 | tf_op jit(solution)/shard_map/psum | solution.py:39
  265.3 14.1 %psum.61 = f32[128]{0:T(128)S(1)} all-reduce(f32[128]{0:T(128)S(1)} %psum.60), channel_id=1, replica_groups=mesh['sub_0'=4,'sub_1'=4,'sub_2'=2,'grp'=4] {'sub_1'}, use_global_device_ids=true, to_apply=%region_7.8 | all-reduce | flops 128 | bytes 1024 | tf_op jit(solution)/shard_map/psum | solution.py:39
  281.8 10.1 %psum.63 = f32[128]{0:T(128)S(1)} all-reduce(f32[128]{0:T(128)S(1)} %psum.62), channel_id=1, replica_groups=mesh['sub_0'=4,'sub_1'=4,'sub_2'=2,'grp'=4] {'grp'}, use_global_device_ids=true, to_apply=%region_9.10 | all-reduce | flops 128 | bytes 1024 | tf_op jit(solution)/shard_map/psum | solution.py:39
  291.9 3.6 %multiply_add_fusion = (f32[1,128,2048]{2,1,0:T(8,128)}, f32[1,128,2048]{2,1,0:T(8,128)}) fusion(f32[1,128,2048]{2,1,0:T(8,128)} %param.16, f32[1,128,1024]{2,1,0:T(8,128)} %copy-done.8, f32[1,128,1024]{2,1,0:T(8,128)} %copy-done.7, f32[128]{0:T(128)S(1)} %div.23, f32[1,128,2048]{2,1,0:T(8,128)} %param.14, f32[128]{0:T(128)S(1)} %div.18), kind=kLoop, calls=%fused_computation.57 | loop fusion | flops 1310720 | bytes 5243904 | tf_op jit(solution)/shard_map/add | solution.py:188
  (113 shorter events, 62.7 us)
Async XLA Ops:
  0.6 56.3 %copy-start = (bf16[1,96,128,128]{3,2,1,0:T(8,128)(2,1)S(1)}, bf16[1,96,128,128]{3,2,1,0:T(8,128)(2,1)}, u32[]{:S(2)}) copy-start(bf16[1,96,128,128]{3,2,1,0:T(8,128)(2,1)} %param.20) | copy-start | bytes 9437188
  0.6 17.5 %copy-start.18 = (s32[1,4]{1,0:T(1,128)S(1)}, s32[1,4]{1,0:T(1,128)}, u32[]{:S(2)}) copy-start(s32[1,4]{1,0:T(1,128)} %param.18) | copy-start | bytes 52
  2.6 12.7 %collective-permute-start = (f32[1,128,1024]{2,0,1:T(1,128)S(1)}, f32[1,128,1024]{2,0,1:T(1,128)S(1)}, u32[]{:S(2)}, u32[]{:S(2)}) collective-permute-start(f32[1,128,1024]{2,0,1:T(1,128)S(1)} %copy.70), channel_id=1, source_target_pairs={{0,4},{4,8},{8,12},{12,16},{16,20},{20,24},{24,28},{28,32},{32,36}... | collective-permute-start | bytes 1572872 | tf_op jit(solution)/shard_map/ppermute | solution.py:20
  3.3 14.9 %collective-permute-start.1 = (f32[1,128,1024]{2,0,1:T(1,128)S(1)}, f32[1,128,1024]{2,0,1:T(1,128)S(1)}, u32[]{:S(2)}, u32[]{:S(2)}) collective-permute-start(f32[1,128,1024]{2,0,1:T(1,128)S(1)} %copy.71), channel_id=1, source_target_pairs={{0,1},{1,2},{2,3},{3,0},{4,5},{5,6},{6,7},{7,4},{8,9},{9,10},{10,1... | collective-permute-start | bytes 1572872 | tf_op jit(solution)/shard_map/ppermute | solution.py:20
  26.4 2.2 copy-start.2
  95.7 11.9 %collective-permute-start.2 = (f32[1,128,1024]{2,1,0:T(8,128)S(1)}, f32[1,128,1024]{2,1,0:T(8,128)S(1)}, u32[]{:S(2)}, u32[]{:S(2)}) collective-permute-start(f32[1,128,1024]{2,1,0:T(8,128)S(1)} %copy.73), channel_id=1, source_target_pairs={{0,124},{4,0},{8,4},{12,8},{16,12},{20,16},{24,20},{28,24},{32,28}... | collective-permute-start | bytes 1572872 | tf_op jit(solution)/shard_map/ppermute | solution.py:20
  100.9 10.1 %copy-start.5 = (f32[1,128,2048]{2,1,0:T(8,128)S(1)}, f32[1,128,2048]{2,1,0:T(8,128)}, u32[]{:S(2)}) copy-start(f32[1,128,2048]{2,1,0:T(8,128)} %param.16) | copy-start | bytes 3145732
  101.0 9.8 %collective-permute-start.3 = (f32[1,128,1024]{2,1,0:T(8,128)S(1)}, f32[1,128,1024]{2,1,0:T(8,128)S(1)}, u32[]{:S(2)}, u32[]{:S(2)}) collective-permute-start(f32[1,128,1024]{2,1,0:T(8,128)S(1)} %copy.75), channel_id=1, source_target_pairs={{0,3},{1,0},{2,1},{3,2},{4,7},{5,4},{6,5},{7,6},{8,11},{9,8},{10,9... | collective-permute-start | bytes 1572872 | tf_op jit(solution)/shard_map/ppermute | solution.py:20
  107.7 38.5 %copy-start.20 = (f32[128]{0:T(128)S(1)}, f32[128]{0:T(128)}, u32[]{:S(2)}) copy-start(f32[128]{0:T(128)} %param.17) | copy-start | bytes 1540
  147.6 109.8 %copy-start.4 = (f32[1,128,2048]{2,1,0:T(8,128)}, f32[1,128,2048]{2,1,0:T(8,128)S(1)}, u32[]{:S(2)}) copy-start(f32[1,128,2048]{2,1,0:T(8,128)S(1)} %multiply_subtract_fusion) | copy-start | bytes 3145732
  147.7 12.0 %copy-start.9 = (f32[1,128,1024]{2,1,0:T(8,128)}, f32[1,128,1024]{2,1,0:T(8,128)S(1)}, u32[]{:S(2)}) copy-start(f32[1,128,1024]{2,1,0:T(8,128)S(1)} %get-tuple-element.18) | copy-start | bytes 1572868
  147.7 12.0 %copy-start.10 = (f32[1,128,1024]{2,1,0:T(8,128)}, f32[1,128,1024]{2,1,0:T(8,128)S(1)}, u32[]{:S(2)}) copy-start(f32[1,128,1024]{2,1,0:T(8,128)S(1)} %get-tuple-element.19) | copy-start | bytes 1572868
  147.7 12.0 %collective-permute-start.4 = (f32[1,128,1024]{2,1,0:T(8,128)S(1)}, f32[1,128,1024]{2,1,0:T(8,128)S(1)}, u32[]{:S(2)}, u32[]{:S(2)}) collective-permute-start(f32[1,128,1024]{2,1,0:T(8,128)S(1)} %get-tuple-element.18), channel_id=1, source_target_pairs={{0,4},{4,8},{8,12},{12,16},{16,20},{20,24},{24,28},{28,32},{32,36}... | collective-permute-start | bytes 1572872 | tf_op jit(solution)/shard_map/ppermute | solution.py:20
  147.8 14.9 %collective-permute-start.5 = (f32[1,128,1024]{2,1,0:T(8,128)S(1)}, f32[1,128,1024]{2,1,0:T(8,128)}, u32[]{:S(2)}, u32[]{:S(2)}) collective-permute-start(f32[1,128,1024]{2,1,0:T(8,128)S(1)} %get-tuple-element.19), channel_id=1, source_target_pairs={{0,1},{1,2},{2,3},{3,0},{4,5},{5,6},{6,7},{7,4},{8,9},{9,10},{10,1... | collective-permute-start | bytes 1572872 | tf_op jit(solution)/shard_map/ppermute | solution.py:20
  169.2 2.3 copy-start.19
  175.0 11.0 %copy-start.15 = (f32[1,128,128]{2,1,0:T(8,128)S(1)}, f32[1,128,128]{2,1,0:T(8,128)}, u32[]{:S(2)}) copy-start(f32[1,128,128]{2,1,0:T(8,128)} %param.26) | copy-start | bytes 196612
  187.1 10.1 %all-to-all-start = ((f32[4,1,128,128]{3,2,1,0:T(8,128)}), f32[4,1,128,128]{3,2,1,0:T(8,128)S(1)}, u32[]{:S(2)}, u32[]{:S(2)}) async-start(f32[4,1,128,128]{3,2,1,0:T(8,128)} %broadcast_in_dim.2), calls=%async_computation | async-start | bytes 524288 | tf_op jit(solution)/shard_map/all_to_all | solution.py:31
  197.2 11.9 %collective-permute-start.6 = (f32[4,128,128]{2,1,0:T(8,128)S(1)}, f32[4,128,128]{2,1,0:T(8,128)S(1)}, u32[]{:S(2)}, u32[]{:S(2)}) collective-permute-start(f32[4,128,128]{2,1,0:T(8,128)S(1)} %bitcast.120), channel_id=1, source_target_pairs={{0,8},{4,12},{8,16},{12,20},{16,24},{20,28},{24,32},{28,36},{32,40... | collective-permute-start | bytes 786440 | tf_op jit(solution)/shard_map/ppermute | solution.py:20
  198.4 11.2 %collective-permute-start.7 = (f32[4,128,128]{2,1,0:T(8,128)S(1)}, f32[4,128,128]{2,1,0:T(8,128)S(1)}, u32[]{:S(2)}, u32[]{:S(2)}) collective-permute-start(f32[4,128,128]{2,1,0:T(8,128)S(1)} %bitcast.121), channel_id=1, source_target_pairs={{0,4},{4,8},{8,12},{12,16},{16,20},{20,24},{24,28},{28,32},{32,36}... | collective-permute-start | bytes 786440 | tf_op jit(solution)/shard_map/ppermute | solution.py:20
  203.2 11.2 %collective-permute-start.8 = (f32[4,128,128]{2,1,0:T(8,128)S(1)}, f32[4,128,128]{2,1,0:T(8,128)S(1)}, u32[]{:S(2)}, u32[]{:S(2)}) collective-permute-start(f32[4,128,128]{2,1,0:T(8,128)S(1)} %bitcast.122), channel_id=1, source_target_pairs={{0,124},{4,0},{8,4},{12,8},{16,12},{20,16},{24,20},{28,24},{32,28}... | collective-permute-start | bytes 786440 | tf_op jit(solution)/shard_map/ppermute | solution.py:20
  208.3 8.9 %collective-permute-start.9 = (f32[4,128,128]{2,1,0:T(8,128)S(1)}, f32[4,128,128]{2,1,0:T(8,128)S(1)}, u32[]{:S(2)}, u32[]{:S(2)}) collective-permute-start(f32[4,128,128]{2,1,0:T(8,128)S(1)} %bitcast.123), channel_id=1, source_target_pairs={{0,120},{4,124},{8,0},{12,4},{16,8},{20,12},{24,16},{28,20},{32,24... | collective-permute-start | bytes 786440 | tf_op jit(solution)/shard_map/ppermute | solution.py:20
  209.7 9.0 %copy-start.12 = (f32[1,9,128,128]{3,2,1,0:T(8,128)S(1)}, f32[1,9,128,128]{3,2,1,0:T(8,128)}, u32[]{:S(2)}) copy-start(f32[1,9,128,128]{3,2,1,0:T(8,128)} %param.25) | copy-start | bytes 1769476
  217.2 2.6 copy-start.16
  217.2 2.9 copy-start.17
  225.5 3.1 %copy-start.6 = (f32[32,128,128]{2,1,0:T(8,128)S(1)}, f32[32,128,128]{2,1,0:T(8,128)}, u32[]{:S(2)}) copy-start(f32[32,128,128]{2,1,0:T(8,128)} %fusion.37) | copy-start | bytes 6291460
  242.6 9.2 %collective-permute-start.10 = (f32[1,128,1024]{2,1,0:T(8,128)S(1)}, f32[1,128,1024]{2,1,0:T(8,128)S(1)}, u32[]{:S(2)}, u32[]{:S(2)}) collective-permute-start(f32[1,128,1024]{2,1,0:T(8,128)S(1)} %copy.77), channel_id=1, source_target_pairs={{0,124},{4,0},{8,4},{12,8},{16,12},{20,16},{24,20},{28,24},{32,28}... | collective-permute-start | bytes 1572872 | tf_op jit(solution)/shard_map/ppermute | solution.py:20
  245.3 12.0 %collective-permute-start.11 = (f32[1,128,1024]{2,1,0:T(8,128)S(1)}, f32[1,128,1024]{2,1,0:T(8,128)S(1)}, u32[]{:S(2)}, u32[]{:S(2)}) collective-permute-start(f32[1,128,1024]{2,1,0:T(8,128)S(1)} %copy.79), channel_id=1, source_target_pairs={{0,3},{1,0},{2,1},{3,2},{4,7},{5,4},{6,5},{7,6},{8,11},{9,8},{10,9... | collective-permute-start | bytes 1572872 | tf_op jit(solution)/shard_map/ppermute | solution.py:20
  252.0 5.6 %copy-start.7 = (f32[1,128,1024]{2,1,0:T(8,128)}, f32[1,128,1024]{2,1,0:T(8,128)S(1)}, u32[]{:S(2)}) copy-start(f32[1,128,1024]{2,1,0:T(8,128)S(1)} %copy_add_fusion.1) | copy-start | bytes 1572868
  252.0 39.9 %copy-start.21 = (f32[128]{0:T(128)S(1)}, f32[128]{0:T(128)}, u32[]{:S(2)}) copy-start(f32[128]{0:T(128)} %param.17) | copy-start | bytes 1540
  257.4 7.9 %copy-start.8 = (f32[1,128,1024]{2,1,0:T(8,128)}, f32[1,128,1024]{2,1,0:T(8,128)S(1)}, u32[]{:S(2)}) copy-start(f32[1,128,1024]{2,1,0:T(8,128)S(1)} %copy_add_fusion) | copy-start | bytes 1572868
  291.9 3.6 %copy-start.22 = (f32[128]{0:T(128)}, f32[128]{0:T(128)S(1)}, u32[]{:S(2)}) copy-start(f32[128]{0:T(128)S(1)} %psum.63) | copy-start | bytes 1540
  291.9 3.6 %copy-start.1 = (bf16[1,96,128,128]{3,2,1,0:T(8,128)(2,1)S(1)}, bf16[1,96,128,128]{3,2,1,0:T(8,128)(2,1)}, u32[]{:S(2)}) copy-start(bf16[1,96,128,128]{3,2,1,0:T(8,128)(2,1)} %param.20) | copy-start | bytes 9437188
  (4 other events, 6.0 us)
where the time goes:
time: 301 us; the launch traced here: 296 us
  matrix products  99.9 us (33%)
  blocking collectives  69.4 us (23%)
  waiting for transfers between devices  58.7 us (20%)
  local copies, waits for them, and re-layouts  28 us (9%)
  starting transfers between devices  23.2 us (8%)
  other arithmetic  15.1 us (5%)
    psum x8, blocking collectives, by_axis(): return functools.reduce(lax.psum, axes, array)  69.4 us
    ppermute x12, waiting for transfers between devices, shifted(): return lax.ppermute(value, axis, pairs)  52.7 us
    dot_general x1, matrix products, condensed(): jnp.einsum('lib,ibk->lik', paired, couple, precision=highest_precision)  21.7 us
    ppermute x12, starting transfers between devices, shifted(): return lax.ppermute(value, axis, pairs)  19.8 us
    dot_general x1, matrix products, precondition(): jnp.einsum('lcb,cb->lc', picked, primal_rows, precision=highest_precision)  11 us
    dot_general x2, matrix products, place_faces(): jnp.einsum('dk,dlf->lkf', slot_onehot, directed, precision=highest_precis...  9.92 us
    dot_general x1, matrix products, condensed(): jnp.einsum('lim,ikm->lik', middle, dirichlet, precision=highest_precision)  8.47 us
    dot_general x1, matrix products, condensed(): jnp.einsum('lik,ibk->lib', solved, couple, precision=highest_precision)  8.36 us
  transfers between devices with their start and end apart: 13, of which 12 were waited for; matrix products, arithmetic and copies ran while one was open for 3% of the time, Pallas kernels for 0%

commit v1 on v0

v1 whole, which is shorter than its diff:
```python
import functools

import jax
import jax.numpy as jnp
from jax import lax
from jax.experimental import pallas as pl
from jax.experimental.pallas import tpu as pltpu
from jax.sharding import PartitionSpec as P

F32 = jnp.float32
BF16 = jnp.bfloat16
MESH = pl.DeviceIdType.MESH

N_SUB = 32
N_GRP = 4
ROW = 8
N_X = N_SUB // ROW
W = 128
FB = 8
FACE = FB * W
REACH = 2


def split(x):
    hi = x.astype(BF16)
    lo = (x - hi.astype(F32)).astype(BF16)
    return hi, lo


def wide(x):
    return jnp.concatenate(split(x), 1)


def mm(x, w):
    return lax.dot_general(x, w, (((1,), (0,)), ((), ())), preferred_element_type=F32)


def mmt(x, w):
    return lax.dot_general(x, w, (((1,), (1,)), ((), ())), preferred_element_type=F32)


def mm3(x, w):
    xh, xl = split(x)
    wh, wl = split(w)
    return mm(jnp.concatenate([xh, xl], 1), jnp.concatenate([wh, wh], 0)) + mm(xh, wl)


def cols(b):
    return pl.ds(b * W, W)


def kernel(
    sol_hbm, res_hbm, dir_hbm, rp_ref, slots, coup_hbm, diri_hbm, face_hbm, neum_hbm, pblk_ref, basis_hbm, cmat_hbm,
    cinv_hbm, patt,
    nsol_hbm, nres_hbm, ndir_hbm, nprod_ref,
    coup, diri, face, neum, basis, cmat, cinv, sol, res,
    uf, uhl, yy, ss, c2, nr, prec, nst, nf, bms, bmr, nrel, pbm, crs, crr, cis, cir, ownc, win, cors, corr_in,
    avec, cres, z2, ar_y, ar_z, ar_x,
    lsem, osem, dsend, drecv, nsend, nrecv, bsend, brecv, crsend, crrecv, cisend, cirecv, c2send, c2recv,
    wysend, wssend, wrecv, cosend, corecv, ysend, yrecv, zsend, zrecv, xsend, xrecv,
):
    i = lax.axis_index("sub")
    g = lax.axis_index("grp")
    row = i // ROW
    col = i % ROW

    def at_sub(k):
        return lax.rem(i + k + N_SUB, N_SUB)

    def at_grp(k):
        return lax.rem(g + k + N_GRP, N_GRP)

    def dev(s, t):
        return {"sub": s, "grp": t}

    neighbor = [dev(at_sub(-1), g), dev(at_sub(1), g), dev(i, at_grp(-1)), dev(i, at_grp(1))]
    y_peers = [dev(i, at_grp(k)) for k in range(1, N_GRP)]
    z_peers = [dev(row * ROW + lax.rem(col + k, ROW), g) for k in range(1, ROW)]
    x_peers = [dev(lax.rem(row + k, N_X) * ROW + col, g) for k in range(1, N_X)]
    reach = [k for k in range(-REACH, REACH + 1) if k != 0]
    s_peers = [dev(at_sub(k), g) for k in reach]

    local = []

    def load(src, dst):
        copy = pltpu.make_async_copy(src, dst, lsem.at[len(local)])
        copy.start()
        local.append(copy)
        return copy

    l_neum = load(neum_hbm.at[0], neum)
    l_basis = load(basis_hbm.at[0], basis)
    l_dir = [load(dir_hbm.at[0, :, pl.ds(f * FACE, FACE)], uf.at[2 * f + 1]) for f in range(2)]
    l_res = [load(res_hbm.at[0, :, pl.ds(f * FACE, FACE)], res.at[f]) for f in range(2)]
    l_face = load(face_hbm.at[0], face)
    l_coup = load(coup_hbm.at[0], coup)
    l_diri = load(diri_hbm.at[0], diri)
    l_cinv = load(cinv_hbm.at[0], cinv)
    l_cmat = load(cmat_hbm.at[0], cmat)
    l_sol = [load(sol_hbm.at[0, :, pl.ds(f * FACE, FACE)], sol.at[f]) for f in range(2)]

    barrier = pltpu.get_barrier_semaphore()
    everyone = y_peers + z_peers + x_peers + s_peers
    for peer in everyone:
        pl.semaphore_signal(barrier, inc=1, device_id=peer, device_id_type=MESH)
    pl.semaphore_wait(barrier, len(everyone))

    sent = []

    def send(src, dst, send_sem, recv_sem, peer):
        copy = pltpu.make_async_remote_copy(
            src_ref=src, dst_ref=dst, send_sem=send_sem, recv_sem=recv_sem, device_id=peer, device_id_type=MESH
        )
        copy.start()
        sent.append(copy)

    def arrived(ref, send_sem, recv_sem):
        pltpu.make_async_remote_copy(
            src_ref=ref, dst_ref=ref, send_sem=send_sem, recv_sem=recv_sem, device_id=neighbor[0], device_id_type=MESH
        ).wait_recv()

    for f in (1, 0):
        send(
            dir_hbm.at[0, :, pl.ds(f * FACE, FACE)], uf.at[2 * f], dsend.at[f], drecv.at[f], neighbor[2 * f + 1]
        )

    l_basis.wait()
    pb_row = pblk_ref[...].astype(F32)
    pbm[...] = jnp.transpose(jnp.broadcast_to(pb_row, (W, W)))
    basis_f = basis[...].astype(F32)
    for d in range(4):
        base = (slots[0, d] * FB).astype(F32)
        bms[d, 0:W, :] = basis_f
        bms[d, W : W + 8, :] = jnp.broadcast_to(pb_row - base, (8, W))
        send(bms.at[d], bmr.at[d ^ 1], bsend.at[d], brecv.at[d ^ 1], neighbor[d])

    l_neum.wait()
    for f in (1, 0):
        start = slots[0, 2 * f] * FB

        def to_f32(b, carry, f=f, start=start):
            nst[f, b] = neum[start + b].astype(F32)
            return carry

        lax.fori_loop(0, FB, to_f32, 0)
        send(nst.at[f], nf.at[f], nsend.at[f], nrecv.at[f], neighbor[2 * f])

    for d in range(4):
        arrived(bmr.at[d], bsend.at[d], brecv.at[d])
        nrel[d] = jnp.transpose(jnp.broadcast_to(bmr[d, W : W + 1, :], (W, W)))

    def own_mask(d, b):
        number = (slots[0, d] * FB + b).astype(F32)
        return jnp.where(pbm[...] == number, basis[...].astype(F32), 0.0).astype(BF16)

    def nb_mask(d, b):
        return jnp.where(nrel[d] == float(b), bmr[d, 0:W, :], 0.0).astype(BF16)

    def coarse_pair(read, d):
        total = None
        for b in range(FB):
            both = jnp.concatenate([own_mask(d, b), nb_mask(d, b)], 0)
            part = mmt(wide(read(b)), jnp.concatenate([both, both], 1))
            total = part if total is None else total + part
        return total

    for copy in l_res:
        copy.wait()
    ownc[...] = jnp.zeros_like(ownc)

    def coarse_of_residual(f, carry):
        pair = coarse_pair(lambda b: res[f, :, cols(b)], 2 * f + 1)
        ownc[0] += pair[:, :W]
        crs[f] = pair[:, W:]
        return carry

    lax.fori_loop(0, 2, coarse_of_residual, 0)
    for f in range(2):
        send(crs.at[f], crr.at[f], crsend.at[f], crrecv.at[f], neighbor[2 * f + 1])

    for copy in l_dir:
        copy.wait()
    l_face.wait()
    l_coup.wait()
    l_diri.wait()

    def interior(jobs):
        first = []
        for lhs, n in jobs:
            two = mm(lhs, coup[n])
            first.append(wide(two[:W] + two[W:]))
        second = []
        for x, (_, n) in zip(first, jobs):
            m = diri[n]
            second.append(wide(mm(x, jnp.concatenate([m, m], 0))))
        third = []
        for x, (_, n) in zip(second, jobs):
            m = diri[n]
            third.append(wide(mmt(x, jnp.concatenate([m, m], 1))))
        out = []
        for x, (_, n) in zip(third, jobs):
            m = coup[n]
            out.append(mmt(x, jnp.concatenate([m, m], 1)))
        return out

    inside = [(q, b) for q in range(3) for b in range(FB - 1 - q)]

    def one_direction(step, carry):
        d = lax.rem(2 * step + 1, 5)

        @pl.when(step == 2)
        def _():
            arrived(uf.at[0], dsend.at[0], drecv.at[0])

        @pl.when(step == 3)
        def _():
            arrived(uf.at[2], dsend.at[1], drecv.at[1])

        base = slots[0, d] * FB
        for b in range(FB):
            hi, lo = split(uf[d, :, cols(b)])
            uhl[d, 0:W, cols(b)] = hi
            uhl[d, W : 2 * W, cols(b)] = lo
            m = face[base + b]
            yy[d, :, cols(b)] = mm(jnp.concatenate([hi, lo], 1), jnp.concatenate([m, m], 0))
        for k in range(0, len(inside), 6):
            group = inside[k : k + 6]
            jobs = [
                (
                    jnp.concatenate([uhl[d, :, cols(b)], uhl[d, :, cols(b + q + 1)]], 1),
                    q * 4 * FB + base + b,
                )
                for q, b in group
            ]
            for (q, b), out in zip(group, interior(jobs)):
                yy[d, :, cols(b)] += out[:, :W]
                yy[d, :, cols(b + q + 1)] += out[:, W:]
        return carry

    lax.fori_loop(0, 4, one_direction, 0)

    def direction_of(slot):
        where = jnp.int32(0)
        for d in range(1, 4):
            where = jnp.where(slots[0, d] == slot, jnp.int32(d), where)
        return where

    across = [(q, b) for q in range(3) for b in range(FB - 1 - q, FB)]

    def straddling(d, carry):
        slot = slots[0, d]
        after = direction_of(lax.rem(slot + 1, 4))
        jobs = [
            (
                jnp.concatenate([uhl[d, :, cols(b)], uhl[after, :, cols(b + q + 1 - FB)]], 1),
                q * 4 * FB + slot * FB + b,
            )
            for q, b in across
        ]
        tails = [None] * 3
        for (q, b), out in zip(across, interior(jobs)):
            yy[d, :, cols(b)] += out[:, :W]
            m = b + q + 1 - FB
            tails[m] = out[:, W:] if tails[m] is None else tails[m] + out[:, W:]
        for m in range(3):
            ss[d, :, cols(m)] = tails[m]
        return carry

    lax.fori_loop(0, 4, straddling, 0)

    for d in range(4):
        before = direction_of(lax.rem(slots[0, d] + 3, 4))
        for m in range(3):
            yy[d, :, cols(m)] += ss[before, :, cols(m)]

    for f in (1, 0):
        send(yy.at[2 * f], c2.at[f], c2send.at[f], c2recv.at[f], neighbor[2 * f])

    def folded(x):
        return jnp.sum(jnp.transpose(x).reshape(W // 8, 8, W), axis=0)

    stages = (
        (ar_y, ysend, yrecv, N_GRP, g, y_peers),
        (ar_z, zsend, zrecv, ROW, col, z_peers),
        (ar_x, xsend, xrecv, N_X, row, x_peers),
    )

    def stage_send(which, stage, value):
        buf, ssem, rsem, count, me, peers = stages[stage]
        buf[which, me] = value
        for k, peer in enumerate(peers):
            send(buf.at[which, me], buf.at[which, me], ssem.at[which, k], rsem.at[which, me], peer)

    def stage_wait(which, stage):
        buf, ssem, rsem, count, me, peers = stages[stage]
        for k in range(1, count):
            other = lax.rem(me + k, count)
            arrived(buf.at[which, other], ssem.at[which, 0], rsem.at[which, other])
        total = buf[which, 0]
        for k in range(1, count):
            total = total + buf[which, k]
        return total

    def curve(d, acc):
        for b in range(FB):
            acc = acc + uf[d, :, cols(b)] * yy[d, :, cols(b)]
        return acc

    stage_send(0, 0, folded(lax.fori_loop(0, 4, curve, jnp.zeros((W, W), F32))))

    def coarse_of_image(d, carry):
        pair = coarse_pair(lambda b: yy[d, :, cols(b)], d)
        ownc[1] += pair[:, :W]
        cis[d] = pair[:, W:]
        return carry

    lax.fori_loop(0, 4, coarse_of_image, 0)
    for d in (2, 3, 0, 1):
        send(cis.at[d], cir.at[d ^ 1], cisend.at[d], cirecv.at[d ^ 1], neighbor[d])

    stage_send(0, 1, stage_wait(0, 0))
    stage_send(0, 2, stage_wait(0, 1))
    rp_row = rp_ref[...]
    curvature = jnp.sum(stage_wait(0, 2), axis=0, keepdims=True)
    avec[...] = jnp.transpose(jnp.broadcast_to(rp_row / curvature, (W, W)))

    for f in range(2):
        arrived(crr.at[f], crsend.at[f], crrecv.at[f])
    for d in range(4):
        arrived(cir.at[d], cisend.at[d], cirecv.at[d])
    l_cinv.wait()
    image_part = ownc[1] + ((cir[0] + cir[1]) + (cir[2] + cir[3]))
    residual_part = ownc[0] + (crr[0] + crr[1])
    cres[0] = 0.5 * (residual_part - avec[...] * image_part)
    win[REACH, g] = mm3(cres[0], cinv[...])
    for k, peer in enumerate(y_peers):
        send(win.at[REACH, g], win.at[REACH, g], wysend.at[k], wrecv.at[REACH, g], peer)

    def forward(k):
        piece = at_grp(k)
        for n, (step, peer) in enumerate(zip(reach, s_peers)):
            send(
                win.at[REACH, piece], win.at[REACH - step, piece], wssend.at[k, n], wrecv.at[REACH - step, piece], peer
            )

    forward(0)

    for copy in l_sol:
        copy.wait()
    outs = []

    def store(src, dst):
        copy = pltpu.make_async_copy(src, dst, osem.at[len(outs)])
        copy.start()
        outs.append(copy)

    z2[...] = jnp.zeros_like(z2)

    def own_face(f):
        a = avec[...]
        base = slots[0, 2 * f + 1] * FB
        acc = z2[...]
        for b in range(FB):
            sol[f, :, cols(b)] += a * uf[2 * f + 1, :, cols(b)]
            new = res[f, :, cols(b)] - a * (yy[2 * f + 1, :, cols(b)] + c2[f, :, cols(b)])
            nr[f, :, cols(b)] = new
            mine = neum[base + b]
            theirs = nf[f, b].astype(BF16)
            both = jnp.concatenate([mine, theirs], 1)
            z = mm(wide(0.5 * new), jnp.concatenate([both, both], 0))
            acc = acc + (z[:, :W] * z[:, :W] + z[:, W:] * z[:, W:])
            lhs = jnp.concatenate([wide(z[:, :W]), wide(z[:, W:])], 1)
            prec[f, :, cols(b)] = mmt(lhs, jnp.concatenate([mine, mine, theirs, theirs], 1))
        z2[...] = acc

    arrived(c2.at[0], c2send.at[0], c2recv.at[0])
    arrived(nf.at[0], nsend.at[0], nrecv.at[0])
    own_face(0)
    for k in range(1, N_GRP):
        piece = at_grp(k)
        arrived(win.at[REACH, piece], wysend.at[0], wrecv.at[REACH, piece])
        forward(k)
    arrived(c2.at[1], c2send.at[1], c2recv.at[1])
    arrived(nf.at[1], nsend.at[1], nrecv.at[1])
    own_face(1)
    for f in range(2):
        store(sol.at[f], nsol_hbm.at[0, :, pl.ds(f * FACE, FACE)])
        store(nr.at[f], nres_hbm.at[0, :, pl.ds(f * FACE, FACE)])

    for k in range(N_GRP):
        piece = at_grp(k)
        for step in reach:
            arrived(win.at[REACH - step, piece], wssend.at[0, 0], wrecv.at[REACH - step, piece])
    l_cmat.wait()
    adjacent = None
    for k in range(9):
        entry = patt[0, k]
        place = jnp.minimum(lax.rem(entry // N_GRP - i + REACH + N_SUB, N_SUB), 2 * REACH)
        part = mm3(win[place, lax.rem(entry, N_GRP)], cmat[k])
        adjacent = part if adjacent is None else adjacent + part
    corr = win[REACH, g] + mm3(cres[0] - adjacent, cinv[...])
    cors[...] = corr
    for f in (1, 0):
        send(cors, corr_in.at[f], cosend.at[f], corecv.at[f], neighbor[2 * f])
    stage_send(1, 0, folded(z2[...] + corr * cres[0]))

    mine_w = wide(corr)
    for f in range(2):
        arrived(corr_in.at[f], cosend.at[f], corecv.at[f])

    def spread_back(f, carry):
        lhs = jnp.concatenate([wide(cors[...]), wide(corr_in[f])], 1)
        for b in range(FB):
            own = own_mask(2 * f + 1, b)
            other = nb_mask(2 * f + 1, b)
            back = mm(lhs, jnp.concatenate([own, own, other, other], 0))
            prec[f, :, cols(b)] = 0.5 * (prec[f, :, cols(b)] + back)
        return carry

    lax.fori_loop(0, 2, spread_back, 0)

    stage_send(1, 1, stage_wait(1, 0))
    stage_send(1, 2, stage_wait(1, 1))
    product = jnp.sum(stage_wait(1, 2), axis=0, keepdims=True)
    nprod_ref[...] = product
    avec[...] = jnp.transpose(jnp.broadcast_to(product / rp_row, (W, W)))

    def new_direction(f, carry):
        a = avec[...]
        for b in range(FB):
            prec[f, :, cols(b)] += a * uf[2 * f + 1, :, cols(b)]
        return carry

    lax.fori_loop(0, 2, new_direction, 0)
    for f in range(2):
        store(prec.at[f], ndir_hbm.at[0, :, pl.ds(f * FACE, FACE)])
    for copy in sent:
        copy.wait_send()
    for copy in outs:
        copy.wait()


def shards(
    solution,
    residual,
    direction,
    residual_product,
    neighbor_slots,
    coupling,
    dirichlet_factor,
    face_block,
    neumann_factor,
    primal_block,
    primal_basis,
    coarse_matrix,
    coarse_block_inverse,
    coarse_pattern,
):
    hbm = pl.BlockSpec(memory_space=pl.ANY)
    vmem = pl.BlockSpec(memory_space=pltpu.VMEM)
    smem = pl.BlockSpec(memory_space=pltpu.SMEM)
    dma = pltpu.SemaphoreType.DMA
    big = jax.ShapeDtypeStruct((1, W, 2 * FACE), F32)
    nsol, nres, ndir, nprod = pl.pallas_call(
        kernel,
        out_shape=(big, big, big, jax.ShapeDtypeStruct((1, W), F32)),
        in_specs=[hbm, hbm, hbm, vmem, smem, hbm, hbm, hbm, hbm, vmem, hbm, hbm, hbm, smem],
        out_specs=(hbm, hbm, hbm, vmem),
        scratch_shapes=[
            pltpu.VMEM((96, 2 * W, W), BF16),
            pltpu.VMEM((96, W, W), BF16),
            pltpu.VMEM((32, W, W), BF16),
            pltpu.VMEM((32, W, W), BF16),
            pltpu.VMEM((W, W), BF16),
            pltpu.VMEM((9, W, W), F32),
            pltpu.VMEM((W, W), F32),
            pltpu.VMEM((2, W, FACE), F32),
            pltpu.VMEM((2, W, FACE), F32),
            pltpu.VMEM((4, W, FACE), F32),
            pltpu.VMEM((4, 2 * W, FACE), BF16),
            pltpu.VMEM((4, W, FACE), F32),
            pltpu.VMEM((4, W, 3 * W), F32),
            pltpu.VMEM((2, W, FACE), F32),
            pltpu.VMEM((2, W, FACE), F32),
            pltpu.VMEM((2, W, FACE), F32),
            pltpu.VMEM((2, FB, W, W), F32),
            pltpu.VMEM((2, FB, W, W), F32),
            pltpu.VMEM((4, W + 8, W), F32),
            pltpu.VMEM((4, W + 8, W), F32),
            pltpu.VMEM((4, W, W), F32),
            pltpu.VMEM((W, W), F32),
            pltpu.VMEM((2, W, W), F32),
            pltpu.VMEM((2, W, W), F32),
            pltpu.VMEM((4, W, W), F32),
            pltpu.VMEM((4, W, W), F32),
            pltpu.VMEM((2, W, W), F32),
            pltpu.VMEM((2 * REACH + 1, N_GRP, W, W), F32),
            pltpu.VMEM((W, W), F32),
            pltpu.VMEM((2, W, W), F32),
            pltpu.VMEM((W, W), F32),
            pltpu.VMEM((1, W, W), F32),
            pltpu.VMEM((W, W), F32),
            pltpu.VMEM((2, N_GRP, 8, W), F32),
            pltpu.VMEM((2, ROW, 8, W), F32),
            pltpu.VMEM((2, N_X, 8, W), F32),
            dma((13,)),
            dma((6,)),
            dma((2,)), dma((2,)),
            dma((2,)), dma((2,)),
            dma((4,)), dma((4,)),
            dma((2,)), dma((2,)),
            dma((4,)), dma((4,)),
            dma((2,)), dma((2,)),
            dma((3,)), dma((N_GRP, 4)), dma((2 * REACH + 1, N_GRP)),
            dma((2,)), dma((2,)),
            dma((2, 3)), dma((2, N_GRP)),
            dma((2, 7)), dma((2, ROW)),
            dma((2, 3)), dma((2, N_X)),
        ],
        compiler_params=pltpu.CompilerParams(
            collective_id=0, has_side_effects=True, vmem_limit_bytes=60 * 1024 * 1024
        ),
        name="pcg_step",
    )(
        solution,
        residual,
        direction,
        residual_product.reshape(1, W),
        neighbor_slots,
        coupling,
        dirichlet_factor,
        face_block,
        neumann_factor,
        primal_block,
        primal_basis,
        coarse_matrix,
        coarse_block_inverse,
        coarse_pattern,
    )
    return nsol, nres, ndir, nprod.reshape(W)


def solution(mesh):
    both = ("sub", "grp")

    def split_first(rank):
        return P(both, *([None] * (rank - 1)))

    return jax.shard_map(
        shards,
        mesh=mesh,
        in_specs=(
            split_first(3), split_first(3), split_first(3), P(), split_first(2), split_first(4), split_first(4),
            split_first(4), split_first(4), split_first(2), split_first(3), split_first(4), split_first(3),
            split_first(2),
        ),
        out_specs=(split_first(3), split_first(3), split_first(3), P()),
        check_vma=False,
    )
```

time: 301 us -> 93.7 us (0.31); the launches traced: 296 us -> 93.4 us
  matrix products: 99.9 us -> 0 us
  Pallas kernels: 0 us -> 85.3 us
  blocking collectives: 69.4 us -> 0 us
  waiting for transfers between devices: 58.7 us -> 0 us
  starting transfers between devices: 23.2 us -> 0 us
  local copies, waits for them, and re-layouts: 28 us -> 7.4 us
  other arithmetic: 15.1 us -> 0 us
    dot_general x18 -> x0, matrix products: 99.9 us -> none  [the longest x1 21.7 us: condensed(): jnp.einsum('lib,ibk->lik', paired, couple, precision=highest_precision)]
    pallas_call x0 -> x1, Pallas kernels: none -> 85.3 us  [shards(): pl.pallas_call(kernel, out_shape=(big, big, big, jax.ShapeDtypeStruct((1,...]
    psum x8 -> x0, blocking collectives: 69.4 us -> none  [by_axis(): return functools.reduce(lax.psum, axes, array)]
    ppermute x12 -> x0, waiting for transfers between devices: 52.7 us -> none  [shifted(): return lax.ppermute(value, axis, pairs)]
    ppermute x12 -> x0, starting transfers between devices: 19.8 us -> none  [shifted(): return lax.ppermute(value, axis, pairs)]
    reshape x3 -> x0, local copies, waits for them, and re-layouts: 9.66 us -> none  [the longest x2 6.59 us: collect(): placed = local_part.reshape(load_count, 4, -1)]
    slice x16 -> x0, local copies, waits for them, and re-layouts: 7.98 us -> none  [the longest x2 3.06 us: collect(): owned_sub = directed[1][None] + to_sub]
    all_to_all x1 -> x0, waiting for transfers between devices: 5.96 us -> none  [from_everyone(): return lax.all_to_all(copies, axis, split_axis=0, concat_axis=0, tiled=True)]
  transfers between devices with their start and end apart: 13 -> 0, of which waited for: 12 -> 0; matrix products, arithmetic and copies ran while one was open for 3% -> 0% of each run, Pallas kernels for 0% -> 0%
where the time goes in v1:
time: 93.7 us; the launch traced here: 93.4 us
  Pallas kernels  85.3 us (91%)
  local copies, waits for them, and re-layouts  7.4 us (8%)
    pallas_call x1, Pallas kernels, shards(): pl.pallas_call(kernel, out_shape=(big, big, big, jax.ShapeDtypeStruct((1,...  85.3 us
    unnamed x6, local copies, waits for them, and re-layouts  7.4 us

profile of v1, /device:TPU:0, one launch (start us, length us, event | category | flops | bytes accessed | tf_op | source)
XLA Modules:
  0.0 93.4 jit_solution(17439461513215303506)
XLA Ops:
  0.6 85.3 %pcg_step.1 = (f32[1,128,2048]{2,1,0:T(8,128)}, f32[1,128,2048]{2,1,0:T(8,128)}, f32[1,128,2048]{2,1,0:T(8,128)}, f32[1,128]{1,0:T(1,128)}) custom-call(f32[1,128,2048]{2,1,0:T(8,128)} %sol_hbm.1, f32[1,128,2048]{2,1,0:T(8,128)} %res_hbm.1, f32[1,128,2048]{2,1,0:T(8,128)} %dir_hbm.1, f32[1,128]{1,0:T(1,128)} %bitcast.2, s32[1,4]{1,0:T(1,128)} %slots.1, ...), custom_call_target="tpu_custom_call" | custom-call | tf_op jit(solution)/shard_map/pcg_step/pallas_call | solution.py:464
  86.0 0.0 copy-start
  86.0 2.3 %copy.22 = f32[1,128,2048]{2,1,0:T(8,128)} copy(f32[1,128,2048]{2,1,0:T(8,128)} %get-tuple-element.16) | data formatting | bytes 2097152
  88.3 2.3 %copy.23 = f32[1,128,2048]{2,1,0:T(8,128)} copy(f32[1,128,2048]{2,1,0:T(8,128)} %get-tuple-element.17) | data formatting | bytes 2097152
  90.6 2.3 %copy.24 = f32[1,128,2048]{2,1,0:T(8,128)} copy(f32[1,128,2048]{2,1,0:T(8,128)} %get-tuple-element.18) | data formatting | bytes 2097152
  92.9 0.0 copy-done
  92.9 0.5 copy.25
Async XLA Ops:
  86.0 6.9 %copy-start = (f32[1,128]{1,0:T(1,128)S(1)}, f32[1,128]{1,0:T(1,128)}, u32[]{:S(2)}) copy-start(f32[1,128]{1,0:T(1,128)} %get-tuple-element.11) | copy-start | bytes 1540

commit v2 on v1

--- a/solution.py
+++ b/solution.py
@@ -50,11 +50,11 @@
 
 
 def kernel(
-    sol_hbm, res_hbm, dir_hbm, rp_ref, slots, coup_hbm, diri_hbm, face_hbm, neum_hbm, pblk_ref, basis_hbm, cmat_hbm,
+    res_hbm, dir_hbm, rp_ref, slots, coup_hbm, diri_hbm, face_hbm, neum_hbm, pblk_ref, basis_hbm, cmat_hbm,
     cinv_hbm, patt,
-    nsol_hbm, nres_hbm, ndir_hbm, nprod_ref,
-    coup, diri, face, neum, basis, cmat, cinv, sol, res,
-    uf, uhl, yy, ss, c2, nr, prec, nst, nf, bms, bmr, nrel, pbm, crs, crr, cis, cir, ownc, win, cors, corr_in,
+    nr_hbm, prec_hbm, rows_ref,
+    coup, diri, face, neum, basis, cmat, cinv, res,
+    uf, uhl, yy, tt, ss, c2, nr, prec, nst, nf, bms, bmr, nrel, pbm, crs, crr, cis, cir, ownc, win, cors, corr_in,
     avec, cres, z2, ar_y, ar_z, ar_x,
     lsem, osem, dsend, drecv, nsend, nrecv, bsend, brecv, crsend, crrecv, cisend, cirecv, c2send, c2recv,
     wysend, wssend, wrecv, cosend, corecv, ysend, yrecv, zsend, zrecv, xsend, xrecv,
@@ -97,7 +97,6 @@
     l_diri = load(diri_hbm.at[0], diri)
     l_cinv = load(cinv_hbm.at[0], cinv)
     l_cmat = load(cmat_hbm.at[0], cmat)
-    l_sol = [load(sol_hbm.at[0, :, pl.ds(f * FACE, FACE)], sol.at[f]) for f in range(2)]
 
     barrier = pltpu.get_barrier_semaphore()
     everyone = y_peers + z_peers + x_peers + s_peers
@@ -119,21 +118,31 @@
             src_ref=ref, dst_ref=ref, send_sem=send_sem, recv_sem=recv_sem, device_id=neighbor[0], device_id_type=MESH
         ).wait_recv()
 
-    for f in (1, 0):
+    half = FACE // 2
+    for h in range(2):
         send(
-            dir_hbm.at[0, :, pl.ds(f * FACE, FACE)], uf.at[2 * f], dsend.at[f], drecv.at[f], neighbor[2 * f + 1]
+            dir_hbm.at[0, :, pl.ds(FACE + h * half, half)], uf.at[2, :, pl.ds(h * half, half)],
+            dsend.at[h], drecv.at[h], neighbor[3],
         )
+    send(dir_hbm.at[0, :, pl.ds(0, FACE)], uf.at[0], dsend.at[2], drecv.at[2], neighbor[1])
 
     l_basis.wait()
     pb_row = pblk_ref[...].astype(F32)
     pbm[...] = jnp.transpose(jnp.broadcast_to(pb_row, (W, W)))
     basis_f = basis[...].astype(F32)
     for d in range(4):
-        base = (slots[0, d] * FB).astype(F32)
         bms[d, 0:W, :] = basis_f
-        bms[d, W : W + 8, :] = jnp.broadcast_to(pb_row - base, (8, W))
+        bms[d, W : W + 8, :] = jnp.broadcast_to(pb_row - (slots[0, d] * FB).astype(F32), (8, W))
+
+    def send_basis(d):
         send(bms.at[d], bmr.at[d ^ 1], bsend.at[d], brecv.at[d ^ 1], neighbor[d])
 
+    def basis_arrived(d):
+        arrived(bmr.at[d], bsend.at[d], brecv.at[d])
+        nrel[d] = jnp.transpose(jnp.broadcast_to(bmr[d, W : W + 1, :], (W, W)))
+
+    send_basis(2)
+    send_basis(0)
     l_neum.wait()
     for f in (1, 0):
         start = slots[0, 2 * f] * FB
@@ -144,10 +153,8 @@
 
         lax.fori_loop(0, FB, to_f32, 0)
         send(nst.at[f], nf.at[f], nsend.at[f], nrecv.at[f], neighbor[2 * f])
-
-    for d in range(4):
-        arrived(bmr.at[d], bsend.at[d], brecv.at[d])
-        nrel[d] = jnp.transpose(jnp.broadcast_to(bmr[d, W : W + 1, :], (W, W)))
+    send_basis(3)
+    send_basis(1)
 
     def own_mask(d, b):
         number = (slots[0, d] * FB + b).astype(F32)
@@ -163,20 +170,6 @@
             part = mmt(wide(read(b)), jnp.concatenate([both, both], 1))
             total = part if total is None else total + part
         return total
-
-    for copy in l_res:
-        copy.wait()
-    ownc[...] = jnp.zeros_like(ownc)
-
-    def coarse_of_residual(f, carry):
-        pair = coarse_pair(lambda b: res[f, :, cols(b)], 2 * f + 1)
-        ownc[0] += pair[:, :W]
-        crs[f] = pair[:, W:]
-        return carry
-
-    lax.fori_loop(0, 2, coarse_of_residual, 0)
-    for f in range(2):
-        send(crs.at[f], crr.at[f], crsend.at[f], crrecv.at[f], neighbor[2 * f + 1])
 
     for copy in l_dir:
         copy.wait()
@@ -203,28 +196,19 @@
             out.append(mmt(x, jnp.concatenate([m, m], 1)))
         return out
 
-    inside = [(q, b) for q in range(3) for b in range(FB - 1 - q)]
-
-    def one_direction(step, carry):
-        d = lax.rem(2 * step + 1, 5)
-
-        @pl.when(step == 2)
-        def _():
-            arrived(uf.at[0], dsend.at[0], drecv.at[0])
-
-        @pl.when(step == 3)
-        def _():
-            arrived(uf.at[2], dsend.at[1], drecv.at[1])
-
+    def face_term(d, blocks):
         base = slots[0, d] * FB
-        for b in range(FB):
+        for b in blocks:
             hi, lo = split(uf[d, :, cols(b)])
             uhl[d, 0:W, cols(b)] = hi
             uhl[d, W : 2 * W, cols(b)] = lo
             m = face[base + b]
             yy[d, :, cols(b)] = mm(jnp.concatenate([hi, lo], 1), jnp.concatenate([m, m], 0))
-        for k in range(0, len(inside), 6):
-            group = inside[k : k + 6]
+
+    def within(d, pairs):
+        base = slots[0, d] * FB
+        for k in range(0, len(pairs), 6):
+            group = pairs[k : k + 6]
             jobs = [
                 (
                     jnp.concatenate([uhl[d, :, cols(b)], uhl[d, :, cols(b + q + 1)]], 1),
@@ -235,9 +219,11 @@
             for (q, b), out in zip(group, interior(jobs)):
                 yy[d, :, cols(b)] += out[:, :W]
                 yy[d, :, cols(b + q + 1)] += out[:, W:]
-        return carry
-
-    lax.fori_loop(0, 4, one_direction, 0)
+
+    inside = [(q, b) for q in range(3) for b in range(FB - 1 - q)]
+    early = [(q, b) for q, b in inside if b + q + 1 < FB // 2]
+    late = [(q, b) for q, b in inside if b + q + 1 >= FB // 2]
+    across = [(q, b) for q in range(3) for b in range(FB - 1 - q, FB)]
 
     def direction_of(slot):
         where = jnp.int32(0)
@@ -245,36 +231,71 @@
             where = jnp.where(slots[0, d] == slot, jnp.int32(d), where)
         return where
 
-    across = [(q, b) for q in range(3) for b in range(FB - 1 - q, FB)]
-
-    def straddling(d, carry):
-        slot = slots[0, d]
+    def straddling(p, carry):
+        slot = lax.rem(slots[0, 2] + 1 + p, 4)
+        this = direction_of(slot)
         after = direction_of(lax.rem(slot + 1, 4))
         jobs = [
             (
-                jnp.concatenate([uhl[d, :, cols(b)], uhl[after, :, cols(b + q + 1 - FB)]], 1),
+                jnp.concatenate([uhl[this, :, cols(b)], uhl[after, :, cols(b + q + 1 - FB)]], 1),
                 q * 4 * FB + slot * FB + b,
             )
             for q, b in across
         ]
-        tails = [None] * 3
+        heads, tails = [None] * 3, [None] * 3
         for (q, b), out in zip(across, interior(jobs)):
-            yy[d, :, cols(b)] += out[:, :W]
-            m = b + q + 1 - FB
+            h, m = b - FB + 3, b + q + 1 - FB
+            heads[h] = out[:, :W] if heads[h] is None else heads[h] + out[:, :W]
             tails[m] = out[:, W:] if tails[m] is None else tails[m] + out[:, W:]
         for m in range(3):
-            ss[d, :, cols(m)] = tails[m]
+            tt[p, :, cols(m)] = heads[m]
+            ss[p, :, cols(m)] = tails[m]
         return carry
 
-    lax.fori_loop(0, 4, straddling, 0)
-
+    def first_three(step, carry):
+        d = lax.rem(2 * step + 1, 5)
+
+        @pl.when(step == 2)
+        def _():
+            arrived(uf.at[0], dsend.at[2], drecv.at[2])
+
+        face_term(d, range(FB))
+        within(d, inside)
+        return carry
+
+    lax.fori_loop(0, 3, first_three, 0)
+    lax.fori_loop(0, 2, straddling, 0)
+
+    basis_arrived(3)
+    basis_arrived(1)
+    for copy in l_res:
+        copy.wait()
+    ownc[...] = jnp.zeros_like(ownc)
+
+    def coarse_of_residual(f, carry):
+        pair = coarse_pair(lambda b: res[f, :, cols(b)], 2 * f + 1)
+        ownc[0] += pair[:, :W]
+        crs[f] = pair[:, W:]
+        return carry
+
+    lax.fori_loop(0, 2, coarse_of_residual, 0)
+    for f in range(2):
+        send(crs.at[f], crr.at[f], crsend.at[f], crrecv.at[f], neighbor[2 * f + 1])
+
+    arrived(uf.at[2, :, pl.ds(0, half)], dsend.at[0], drecv.at[0])
+    face_term(2, range(FB // 2))
+    within(2, early)
+    straddling(2, 0)
+    arrived(uf.at[2, :, pl.ds(half, half)], dsend.at[1], drecv.at[1])
+    face_term(2, range(FB // 2, FB))
+    within(2, late)
+    straddling(3, 0)
     for d in range(4):
-        before = direction_of(lax.rem(slots[0, d] + 3, 4))
+        place = lax.rem(slots[0, d] - slots[0, 2] + 7, 4)
+        before = lax.rem(slots[0, d] - slots[0, 2] + 6, 4)
         for m in range(3):
             yy[d, :, cols(m)] += ss[before, :, cols(m)]
-
-    for f in (1, 0):
-        send(yy.at[2 * f], c2.at[f], c2send.at[f], c2recv.at[f], neighbor[2 * f])
+            yy[d, :, cols(FB - 3 + m)] += tt[place, :, cols(m)]
 
     def folded(x):
         return jnp.sum(jnp.transpose(x).reshape(W // 8, 8, W), axis=0)
@@ -308,21 +329,46 @@
 
     stage_send(0, 0, folded(lax.fori_loop(0, 4, curve, jnp.zeros((W, W), F32))))
 
-    def coarse_of_image(d, carry):
+    basis_arrived(0)
+    basis_arrived(2)
+
+    def coarse_of_image(k, carry):
+        d = lax.rem(k + 2, 4)
         pair = coarse_pair(lambda b: yy[d, :, cols(b)], d)
         ownc[1] += pair[:, :W]
         cis[d] = pair[:, W:]
         return carry
 
-    lax.fori_loop(0, 4, coarse_of_image, 0)
-    for d in (2, 3, 0, 1):
+    lax.fori_loop(0, 2, coarse_of_image, 0)
+    for d in (2, 3):
         send(cis.at[d], cir.at[d ^ 1], cisend.at[d], cirecv.at[d ^ 1], neighbor[d])
+    lax.fori_loop(2, 4, coarse_of_image, 0)
+    for d in (0, 1):
+        send(cis.at[d], cir.at[d ^ 1], cisend.at[d], cirecv.at[d ^ 1], neighbor[d])
+
+    quarter = FACE // 4
+
+    def return_piece(f, k):
+        piece = pl.ds(k * quarter, quarter)
+        send(
+            yy.at[2 * f, :, piece], c2.at[f, :, piece], c2send.at[f, k], c2recv.at[f, k], neighbor[2 * f]
+        )
+
+    def returned(f):
+        for k in range(4):
+            piece = pl.ds(k * quarter, quarter)
+            arrived(c2.at[f, :, piece], c2send.at[f, k], c2recv.at[f, k])
 
     stage_send(0, 1, stage_wait(0, 0))
+    return_piece(1, 0)
+    return_piece(1, 1)
     stage_send(0, 2, stage_wait(0, 1))
+    for k in range(4):
+        return_piece(0, k)
     rp_row = rp_ref[...]
     curvature = jnp.sum(stage_wait(0, 2), axis=0, keepdims=True)
-    avec[...] = jnp.transpose(jnp.broadcast_to(rp_row / curvature, (W, W)))
+    step_row = rp_row / curvature
+    avec[...] = jnp.transpose(jnp.broadcast_to(step_row, (W, W)))
 
     for f in range(2):
         arrived(crr.at[f], crsend.at[f], crrecv.at[f])
@@ -344,9 +390,9 @@
             )
 
     forward(0)
-
-    for copy in l_sol:
-        copy.wait()
+    return_piece(1, 2)
+    return_piece(1, 3)
+
     outs = []
 
     def store(src, dst):
@@ -361,7 +407,6 @@
         base = slots[0, 2 * f + 1] * FB
         acc = z2[...]
         for b in range(FB):
-            sol[f, :, cols(b)] += a * uf[2 * f + 1, :, cols(b)]
             new = res[f, :, cols(b)] - a * (yy[2 * f + 1, :, cols(b)] + c2[f, :, cols(b)])
             nr[f, :, cols(b)] = new
             mine = neum[base + b]
@@ -373,19 +418,18 @@
             prec[f, :, cols(b)] = mmt(lhs, jnp.concatenate([mine, mine, theirs, theirs], 1))
         z2[...] = acc
 
-    arrived(c2.at[0], c2send.at[0], c2recv.at[0])
+    returned(0)
     arrived(nf.at[0], nsend.at[0], nrecv.at[0])
     own_face(0)
     for k in range(1, N_GRP):
         piece = at_grp(k)
         arrived(win.at[REACH, piece], wysend.at[0], wrecv.at[REACH, piece])
         forward(k)
-    arrived(c2.at[1], c2send.at[1], c2recv.at[1])
+    returned(1)
     arrived(nf.at[1], nsend.at[1], nrecv.at[1])
     own_face(1)
     for f in range(2):
-        store(sol.at[f], nsol_hbm.at[0, :, pl.ds(f * FACE, FACE)])
-        store(nr.at[f], nres_hbm.at[0, :, pl.ds(f * FACE, FACE)])
+        store(nr.at[f], nr_hbm.at[f])
 
     for k in range(N_GRP):
         piece = at_grp(k)
@@ -418,24 +462,65 @@
         return carry
 
     lax.fori_loop(0, 2, spread_back, 0)
+    for f in range(2):
+        store(prec.at[f], prec_hbm.at[f])
 
     stage_send(1, 1, stage_wait(1, 0))
     stage_send(1, 2, stage_wait(1, 1))
     product = jnp.sum(stage_wait(1, 2), axis=0, keepdims=True)
-    nprod_ref[...] = product
-    avec[...] = jnp.transpose(jnp.broadcast_to(product / rp_row, (W, W)))
-
-    def new_direction(f, carry):
-        a = avec[...]
-        for b in range(FB):
-            prec[f, :, cols(b)] += a * uf[2 * f + 1, :, cols(b)]
-        return carry
-
-    lax.fori_loop(0, 2, new_direction, 0)
-    for f in range(2):
-        store(prec.at[f], ndir_hbm.at[0, :, pl.ds(f * FACE, FACE)])
+    rows_ref[0:1, :] = step_row
+    rows_ref[1:2, :] = product / rp_row
+    rows_ref[2:3, :] = product
     for copy in sent:
         copy.wait_send()
+    for copy in outs:
+        copy.wait()
+
+
+def finish(
+    sol_hbm, dir_hbm, nr_hbm, prec_hbm, rows, nsol_hbm, nres_hbm, ndir_hbm, nprod_ref, sol, dirn, nr, prec, lsem, osem
+):
+    def face(ref, f):
+        return ref.at[0, :, pl.ds(f * FACE, FACE)]
+
+    loads = [
+        [
+            pltpu.make_async_copy(src, dst, lsem.at[f, k])
+            for k, (src, dst) in enumerate(
+                (
+                    (nr_hbm.at[f], nr.at[f]),
+                    (face(sol_hbm, f), sol.at[f]),
+                    (face(dir_hbm, f), dirn.at[f]),
+                    (prec_hbm.at[f], prec.at[f]),
+                )
+            )
+        ]
+        for f in range(2)
+    ]
+    for copy in loads[0] + loads[1]:
+        copy.start()
+    step = jnp.transpose(jnp.broadcast_to(rows[0:1, :], (W, W)))
+    ratio = jnp.transpose(jnp.broadcast_to(rows[1:2, :], (W, W)))
+    nprod_ref[...] = rows[2:3, :]
+    outs = []
+
+    def store(src, dst):
+        copy = pltpu.make_async_copy(src, dst, osem.at[len(outs)])
+        copy.start()
+        outs.append(copy)
+
+    for f in range(2):
+        loads[f][0].wait()
+        store(nr.at[f], face(nres_hbm, f))
+        loads[f][1].wait()
+        loads[f][2].wait()
+        for b in range(FB):
+            sol[f, :, cols(b)] += step * dirn[f, :, cols(b)]
+        store(sol.at[f], face(nsol_hbm, f))
+        loads[f][3].wait()
+        for b in range(FB):
+            prec[f, :, cols(b)] += ratio * dirn[f, :, cols(b)]
+        store(prec.at[f], face(ndir_hbm, f))
     for copy in outs:
         copy.wait()
 
@@ -461,11 +546,12 @@
     smem = pl.BlockSpec(memory_space=pltpu.SMEM)
     dma = pltpu.SemaphoreType.DMA
     big = jax.ShapeDtypeStruct((1, W, 2 * FACE), F32)
-    nsol, nres, ndir, nprod = pl.pallas_call(
+    pair = jax.ShapeDtypeStruct((2, W, FACE), F32)
+    nr, prec, rows = pl.pallas_call(
         kernel,
-        out_shape=(big, big, big, jax.ShapeDtypeStruct((1, W), F32)),
-        in_specs=[hbm, hbm, hbm, vmem, smem, hbm, hbm, hbm, hbm, vmem, hbm, hbm, hbm, smem],
-        out_specs=(hbm, hbm, hbm, vmem),
+        out_shape=(pair, pair, jax.ShapeDtypeStruct((8, W), F32)),
+        in_specs=[hbm, hbm, vmem, smem, hbm, hbm, hbm, hbm, vmem, hbm, hbm, hbm, smem],
+        out_specs=(hbm, hbm, vmem),
         scratch_shapes=[
             pltpu.VMEM((96, 2 * W, W), BF16),
             pltpu.VMEM((96, W, W), BF16),
@@ -475,10 +561,10 @@
             pltpu.VMEM((9, W, W), F32),
             pltpu.VMEM((W, W), F32),
             pltpu.VMEM((2, W, FACE), F32),
-            pltpu.VMEM((2, W, FACE), F32),
             pltpu.VMEM((4, W, FACE), F32),
             pltpu.VMEM((4, 2 * W, FACE), BF16),
             pltpu.VMEM((4, W, FACE), F32),
+            pltpu.VMEM((4, W, 3 * W), F32),
             pltpu.VMEM((4, W, 3 * W), F32),
             pltpu.VMEM((2, W, FACE), F32),
             pltpu.VMEM((2, W, FACE), F32),
@@ -503,14 +589,14 @@
             pltpu.VMEM((2, N_GRP, 8, W), F32),
             pltpu.VMEM((2, ROW, 8, W), F32),
             pltpu.VMEM((2, N_X, 8, W), F32),
-            dma((13,)),
-            dma((6,)),
-            dma((2,)), dma((2,)),
+            dma((11,)),
+            dma((4,)),
+            dma((3,)), dma((3,)),
             dma((2,)), dma((2,)),
             dma((4,)), dma((4,)),
             dma((2,)), dma((2,)),
             dma((4,)), dma((4,)),
-            dma((2,)), dma((2,)),
+            dma((2, 4)), dma((2, 4)),
             dma((3,)), dma((N_GRP, 4)), dma((2 * REACH + 1, N_GRP)),
             dma((2,)), dma((2,)),
             dma((2, 3)), dma((2, N_GRP)),
@@ -522,7 +608,6 @@
         ),
         name="pcg_step",
     )(
-        solution,
         residual,
         direction,
         residual_product.reshape(1, W),
@@ -537,6 +622,21 @@
         coarse_block_inverse,
         coarse_pattern,
     )
+    nsol, nres, ndir, nprod = pl.pallas_call(
+        finish,
+        out_shape=(big, big, big, jax.ShapeDtypeStruct((1, W), F32)),
+        in_specs=[hbm, hbm, hbm, hbm, vmem],
+        out_specs=(hbm, hbm, hbm, vmem),
+        scratch_shapes=[
+            pltpu.VMEM((2, W, FACE), F32),
+            pltpu.VMEM((2, W, FACE), F32),
+            pltpu.VMEM((2, W, FACE), F32),
+            pltpu.VMEM((2, W, FACE), F32),
+            dma((2, 4)),
+            dma((6,)),
+        ],
+        name="finish",
+    )(solution, direction, nr, prec, rows)
     return nsol, nres, ndir, nprod.reshape(W)
 
 

time: 93.7 us -> 71.3 us (0.76)
  Pallas kernels: 85.3 us -> 70.4 us
  local copies, waits for them, and re-layouts: 7.4 us -> 0 us
    pallas_call x1 -> x2, Pallas kernels: 85.3 us -> 70.4 us  [the longest x1 65.9 us: shards(): pl.pallas_call(kernel, out_shape=(pair, pair, jax.ShapeDtypeStruct((8, W)...]
    unnamed x6 -> x0, local copies, waits for them, and re-layouts: 7.4 us -> none
where the time goes in v2:
time: 71.3 us; the launch traced here: 71 us
  Pallas kernels  70.4 us (99%)
    pallas_call x1, Pallas kernels, shards(): pl.pallas_call(kernel, out_shape=(pair, pair, jax.ShapeDtypeStruct((8, W)...  65.9 us
    pallas_call x1, Pallas kernels, shards(): pl.pallas_call(finish, out_shape=(big, big, big, jax.ShapeDtypeStruct((1,...  4.52 us

profile of v2, /device:TPU:0, one launch (start us, length us, event | category | flops | bytes accessed | tf_op | source)
XLA Modules:
  0.0 71.0 jit_solution(5776143950220492959)
XLA Ops:
  0.6 65.9 %pcg_step.1 = (f32[2,128,1024]{2,1,0:T(8,128)}, f32[2,128,1024]{2,1,0:T(8,128)}, f32[8,128]{1,0:T(8,128)}) custom-call(f32[1,128,2048]{2,1,0:T(8,128)} %res_hbm.1, f32[1,128,2048]{2,1,0:T(8,128)} %dir_hbm.3, f32[1,128]{1,0:T(1,128)} %bitcast.2, s32[1,4]{1,0:T(1,128)} %slots.1, bf16[1,96,256,128]{3,2,1,0:T(8,128)(2,1)} %coup_hbm.1, ...), custom_call_target="tpu_custom_call" | custom-call | tf_op jit(solution)/shard_map/pcg_step/pallas_call | solution.py:550
  66.5 4.5 %finish.1 = (f32[1,128,2048]{2,1,0:T(8,128)}, f32[1,128,2048]{2,1,0:T(8,128)}, f32[1,128,2048]{2,1,0:T(8,128)}, f32[1,128]{1,0:T(1,128)}) custom-call(f32[1,128,2048]{2,1,0:T(8,128)} %sol_hbm.1, f32[1,128,2048]{2,1,0:T(8,128)} %dir_hbm.3, f32[2,128,1024]{2,1,0:T(8,128)} %get-tuple-element.11.nr_hbm, f32[2,128,1024]{2,1,0:T(8,128)} %get-tuple-element.12.prec_hbm, ...), custom_call_target="tpu_custom_call" | custom-call | tf_op jit(solution)/shard_map/finish/pallas_call | solution.py:625

commit v3 on v2

--- a/solution.py
+++ b/solution.py
@@ -55,7 +55,7 @@
     nr_hbm, prec_hbm, rows_ref,
     coup, diri, face, neum, basis, cmat, cinv, res,
     uf, uhl, yy, tt, ss, c2, nr, prec, nst, nf, bms, bmr, nrel, pbm, crs, crr, cis, cir, ownc, win, cors, corr_in,
-    avec, cres, z2, ar_y, ar_z, ar_x,
+    avec, z2, ar_y, ar_z, ar_x,
     lsem, osem, dsend, drecv, nsend, nrecv, bsend, brecv, crsend, crrecv, cisend, cirecv, c2send, c2recv,
     wysend, wssend, wrecv, cosend, corecv, ysend, yrecv, zsend, zrecv, xsend, xrecv,
 ):
@@ -79,6 +79,9 @@
     x_peers = [dev(lax.rem(row + k, N_X) * ROW + col, g) for k in range(1, N_X)]
     reach = [k for k in range(-REACH, REACH + 1) if k != 0]
     s_peers = [dev(at_sub(k), g) for k in reach]
+    odd = lax.rem(i, 2)
+    far = [dev(at_sub(REACH), g), dev(at_sub(-REACH), g)]
+    partner = dev(i + 1 - 2 * odd, g)
 
     local = []
 
@@ -119,11 +122,14 @@
         ).wait_recv()
 
     half = FACE // 2
-    for h in range(2):
+
+    def send_half(h):
         send(
             dir_hbm.at[0, :, pl.ds(FACE + h * half, half)], uf.at[2, :, pl.ds(h * half, half)],
             dsend.at[h], drecv.at[h], neighbor[3],
         )
+
+    send_half(0)
     send(dir_hbm.at[0, :, pl.ds(0, FACE)], uf.at[0], dsend.at[2], drecv.at[2], neighbor[1])
 
     l_basis.wait()
@@ -153,9 +159,6 @@
 
         lax.fori_loop(0, FB, to_f32, 0)
         send(nst.at[f], nf.at[f], nsend.at[f], nrecv.at[f], neighbor[2 * f])
-    send_basis(3)
-    send_basis(1)
-
     def own_mask(d, b):
         number = (slots[0, d] * FB + b).astype(F32)
         return jnp.where(pbm[...] == number, basis[...].astype(F32), 0.0).astype(BF16)
@@ -252,20 +255,49 @@
             ss[p, :, cols(m)] = tails[m]
         return carry
 
-    def first_three(step, carry):
-        d = lax.rem(2 * step + 1, 5)
-
-        @pl.when(step == 2)
-        def _():
-            arrived(uf.at[0], dsend.at[2], drecv.at[2])
-
-        face_term(d, range(FB))
-        within(d, inside)
-        return carry
-
-    lax.fori_loop(0, 3, first_three, 0)
-    lax.fori_loop(0, 2, straddling, 0)
-
+    def return_piece(f, k):
+        piece = cols(k)
+        send(
+            yy.at[2 * f, :, piece], c2.at[f, :, piece], c2send.at[f, k], c2recv.at[f, k], neighbor[2 * f]
+        )
+
+    def returned(f):
+        for k in range(FB):
+            piece = cols(k)
+            arrived(c2.at[f, :, piece], c2send.at[f, k], c2recv.at[f, k])
+
+    def first_step(v, value):
+        ownc[v] = value
+        win[v, REACH, g] = mm3(value, cinv[...])
+        for k, peer in enumerate(y_peers):
+            send(win.at[v, REACH, g], win.at[v, REACH, g], wysend.at[v, k], wrecv.at[v, REACH, g], peer)
+        forward(v, 0)
+
+    def forward(v, k):
+        piece = at_grp(k)
+        for n, (place, peer) in enumerate(zip((0, 2 * REACH, 1 + 2 * odd), far + [partner])):
+            send(win.at[v, REACH, piece], win.at[v, place, piece], wssend.at[v, k, n], wrecv.at[v, place, piece], peer)
+
+    def gathered(v):
+        for k in range(1, N_GRP):
+            piece = at_grp(k)
+            arrived(win.at[v, REACH, piece], wysend.at[v, 0], wrecv.at[v, REACH, piece])
+            forward(v, k)
+
+    def relay(v, k):
+        piece = at_grp(k)
+        place, there = 2 * REACH * (1 - odd), 3 - 2 * odd
+        arrived(win.at[v, place, piece], wssend.at[v, 0, 0], wrecv.at[v, place, piece])
+        send(win.at[v, place, piece], win.at[v, there, piece], wssend.at[v, k, 3], wrecv.at[v, there, piece], partner)
+
+    def complete(v):
+        for k in range(N_GRP):
+            piece = at_grp(k)
+            for place in (2 * REACH * odd, 1, 3):
+                arrived(win.at[v, place, piece], wssend.at[v, 0, 0], wrecv.at[v, place, piece])
+
+    face_term(3, range(FB))
+    within(3, inside)
     basis_arrived(3)
     basis_arrived(1)
     for copy in l_res:
@@ -281,21 +313,44 @@
     lax.fori_loop(0, 2, coarse_of_residual, 0)
     for f in range(2):
         send(crs.at[f], crr.at[f], crsend.at[f], crrecv.at[f], neighbor[2 * f + 1])
+    send_half(1)
+    send_basis(3)
+    send_basis(1)
+
+    face_term(1, range(FB))
+    within(1, inside)
 
     arrived(uf.at[2, :, pl.ds(0, half)], dsend.at[0], drecv.at[0])
     face_term(2, range(FB // 2))
     within(2, early)
-    straddling(2, 0)
+    for f in range(2):
+        arrived(crr.at[f], crsend.at[f], crrecv.at[f])
+    l_cinv.wait()
+    first_step(0, ownc[0] + (crr[0] + crr[1]))
+    arrived(uf.at[0], dsend.at[2], drecv.at[2])
+    face_term(0, range(FB))
+    within(0, inside)
+    lax.fori_loop(0, 3, straddling, 0)
+    place = lax.rem(slots[0, 0] - slots[0, 2] + 7, 4)
+    for m in range(3):
+        yy[0, :, cols(FB - 3 + m)] += tt[place, :, cols(m)]
+    for k in range(3, FB):
+        return_piece(0, k)
     arrived(uf.at[2, :, pl.ds(half, half)], dsend.at[1], drecv.at[1])
     face_term(2, range(FB // 2, FB))
     within(2, late)
+    for m in range(3):
+        yy[2, :, cols(m)] += ss[2, :, cols(m)]
+    return_piece(1, 0)
     straddling(3, 0)
     for d in range(4):
         place = lax.rem(slots[0, d] - slots[0, 2] + 7, 4)
         before = lax.rem(slots[0, d] - slots[0, 2] + 6, 4)
         for m in range(3):
-            yy[d, :, cols(m)] += ss[before, :, cols(m)]
-            yy[d, :, cols(FB - 3 + m)] += tt[place, :, cols(m)]
+            if d != 2:
+                yy[d, :, cols(m)] += ss[before, :, cols(m)]
+            if d != 0:
+                yy[d, :, cols(FB - 3 + m)] += tt[place, :, cols(m)]
 
     def folded(x):
         return jnp.sum(jnp.transpose(x).reshape(W // 8, 8, W), axis=0)
@@ -329,6 +384,9 @@
 
     stage_send(0, 0, folded(lax.fori_loop(0, 4, curve, jnp.zeros((W, W), F32))))
 
+    return_piece(1, 1)
+    for k in range(3):
+        return_piece(0, k)
     basis_arrived(0)
     basis_arrived(2)
 
@@ -346,52 +404,24 @@
     for d in (0, 1):
         send(cis.at[d], cir.at[d ^ 1], cisend.at[d], cirecv.at[d ^ 1], neighbor[d])
 
-    quarter = FACE // 4
-
-    def return_piece(f, k):
-        piece = pl.ds(k * quarter, quarter)
-        send(
-            yy.at[2 * f, :, piece], c2.at[f, :, piece], c2send.at[f, k], c2recv.at[f, k], neighbor[2 * f]
-        )
-
-    def returned(f):
-        for k in range(4):
-            piece = pl.ds(k * quarter, quarter)
-            arrived(c2.at[f, :, piece], c2send.at[f, k], c2recv.at[f, k])
-
+    for k in range(2, 5):
+        return_piece(1, k)
     stage_send(0, 1, stage_wait(0, 0))
-    return_piece(1, 0)
-    return_piece(1, 1)
+    gathered(0)
+    for d in range(4):
+        arrived(cir.at[d], cisend.at[d], cirecv.at[d])
+    first_step(1, ownc[1] + ((cir[0] + cir[1]) + (cir[2] + cir[3])))
+    for k in range(5, FB):
+        return_piece(1, k)
     stage_send(0, 2, stage_wait(0, 1))
-    for k in range(4):
-        return_piece(0, k)
+    gathered(1)
+    for k in range(N_GRP):
+        relay(0, k)
     rp_row = rp_ref[...]
     curvature = jnp.sum(stage_wait(0, 2), axis=0, keepdims=True)
     step_row = rp_row / curvature
     avec[...] = jnp.transpose(jnp.broadcast_to(step_row, (W, W)))
-
-    for f in range(2):
-        arrived(crr.at[f], crsend.at[f], crrecv.at[f])
-    for d in range(4):
-        arrived(cir.at[d], cisend.at[d], cirecv.at[d])
-    l_cinv.wait()
-    image_part = ownc[1] + ((cir[0] + cir[1]) + (cir[2] + cir[3]))
-    residual_part = ownc[0] + (crr[0] + crr[1])
-    cres[0] = 0.5 * (residual_part - avec[...] * image_part)
-    win[REACH, g] = mm3(cres[0], cinv[...])
-    for k, peer in enumerate(y_peers):
-        send(win.at[REACH, g], win.at[REACH, g], wysend.at[k], wrecv.at[REACH, g], peer)
-
-    def forward(k):
-        piece = at_grp(k)
-        for n, (step, peer) in enumerate(zip(reach, s_peers)):
-            send(
-                win.at[REACH, piece], win.at[REACH - step, piece], wssend.at[k, n], wrecv.at[REACH - step, piece], peer
-            )
-
-    forward(0)
-    return_piece(1, 2)
-    return_piece(1, 3)
+    relay(1, 0)
 
     outs = []
 
@@ -421,34 +451,37 @@
     returned(0)
     arrived(nf.at[0], nsend.at[0], nrecv.at[0])
     own_face(0)
-    for k in range(1, N_GRP):
-        piece = at_grp(k)
-        arrived(win.at[REACH, piece], wysend.at[0], wrecv.at[REACH, piece])
-        forward(k)
+    relay(1, 1)
+    relay(1, 2)
     returned(1)
     arrived(nf.at[1], nsend.at[1], nrecv.at[1])
     own_face(1)
     for f in range(2):
         store(nr.at[f], nr_hbm.at[f])
 
-    for k in range(N_GRP):
-        piece = at_grp(k)
-        for step in reach:
-            arrived(win.at[REACH - step, piece], wssend.at[0, 0], wrecv.at[REACH - step, piece])
+    relay(1, 3)
+    complete(0)
+    complete(1)
     l_cmat.wait()
+    a = 0.5 * avec[...]
+
+    def combined(place, piece):
+        return 0.5 * win[0, place, piece] - a * win[1, place, piece]
+
     adjacent = None
     for k in range(9):
         entry = patt[0, k]
         place = jnp.minimum(lax.rem(entry // N_GRP - i + REACH + N_SUB, N_SUB), 2 * REACH)
-        part = mm3(win[place, lax.rem(entry, N_GRP)], cmat[k])
+        part = mm3(combined(place, lax.rem(entry, N_GRP)), cmat[k])
         adjacent = part if adjacent is None else adjacent + part
-    corr = win[REACH, g] + mm3(cres[0] - adjacent, cinv[...])
+    coarse_res = 0.5 * ownc[0] - a * ownc[1]
+    corr = combined(REACH, g) + mm3(coarse_res - adjacent, cinv[...])
     cors[...] = corr
+    stage_send(1, 0, folded(z2[...] + corr * coarse_res))
     for f in (1, 0):
         send(cors, corr_in.at[f], cosend.at[f], corecv.at[f], neighbor[2 * f])
-    stage_send(1, 0, folded(z2[...] + corr * cres[0]))
-
-    mine_w = wide(corr)
+    stage_send(1, 1, stage_wait(1, 0))
+    stage_send(1, 2, stage_wait(1, 1))
     for f in range(2):
         arrived(corr_in.at[f], cosend.at[f], corecv.at[f])
 
@@ -465,8 +498,6 @@
     for f in range(2):
         store(prec.at[f], prec_hbm.at[f])
 
-    stage_send(1, 1, stage_wait(1, 0))
-    stage_send(1, 2, stage_wait(1, 1))
     product = jnp.sum(stage_wait(1, 2), axis=0, keepdims=True)
     rows_ref[0:1, :] = step_row
     rows_ref[1:2, :] = product / rp_row
@@ -580,11 +611,10 @@
             pltpu.VMEM((4, W, W), F32),
             pltpu.VMEM((4, W, W), F32),
             pltpu.VMEM((2, W, W), F32),
-            pltpu.VMEM((2 * REACH + 1, N_GRP, W, W), F32),
+            pltpu.VMEM((2, 2 * REACH + 1, N_GRP, W, W), F32),
             pltpu.VMEM((W, W), F32),
             pltpu.VMEM((2, W, W), F32),
             pltpu.VMEM((W, W), F32),
-            pltpu.VMEM((1, W, W), F32),
             pltpu.VMEM((W, W), F32),
             pltpu.VMEM((2, N_GRP, 8, W), F32),
             pltpu.VMEM((2, ROW, 8, W), F32),
@@ -596,8 +626,8 @@
             dma((4,)), dma((4,)),
             dma((2,)), dma((2,)),
             dma((4,)), dma((4,)),
-            dma((2, 4)), dma((2, 4)),
-            dma((3,)), dma((N_GRP, 4)), dma((2 * REACH + 1, N_GRP)),
+            dma((2, FB)), dma((2, FB)),
+            dma((2, 3)), dma((2, N_GRP, 4)), dma((2, 2 * REACH + 1, N_GRP)),
             dma((2,)), dma((2,)),
             dma((2, 3)), dma((2, N_GRP)),
             dma((2, 7)), dma((2, ROW)),

time: 71.3 us -> 66.6 us (0.934)
  Pallas kernels: 70.4 us -> 65.3 us
    pallas_call x1, Pallas kernels: 65.9 us -> 60.8 us  [shards(): pl.pallas_call(kernel, out_shape=(pair, pair, jax.ShapeDtypeStruct((8, W)...]
where the time goes in v3:
time: 66.6 us; the launch traced here: 66.1 us
  Pallas kernels  65.3 us (98%)
  between operations  0.8 us (1%)
    pallas_call x1, Pallas kernels, shards(): pl.pallas_call(kernel, out_shape=(pair, pair, jax.ShapeDtypeStruct((8, W)...  60.8 us
    pallas_call x1, Pallas kernels, shards(): pl.pallas_call(finish, out_shape=(big, big, big, jax.ShapeDtypeStruct((1,...  4.52 us

profile of v3, /device:TPU:0, one launch (start us, length us, event | category | flops | bytes accessed | tf_op | source)
XLA Modules:
  0.0 66.1 jit_solution(10100521761820098738)
XLA Ops:
  0.6 60.8 %pcg_step.1 = (f32[2,128,1024]{2,1,0:T(8,128)}, f32[2,128,1024]{2,1,0:T(8,128)}, f32[8,128]{1,0:T(8,128)}) custom-call(f32[1,128,2048]{2,1,0:T(8,128)} %res_hbm.1, f32[1,128,2048]{2,1,0:T(8,128)} %dir_hbm.3, f32[1,128]{1,0:T(1,128)} %bitcast.2, s32[1,4]{1,0:T(1,128)} %slots.1, bf16[1,96,256,128]{3,2,1,0:T(8,128)(2,1)} %coup_hbm.1, ...), custom_call_target="tpu_custom_call" | custom-call | tf_op jit(solution)/shard_map/pcg_step/pallas_call | solution.py:581
  61.5 4.5 %finish.1 = (f32[1,128,2048]{2,1,0:T(8,128)}, f32[1,128,2048]{2,1,0:T(8,128)}, f32[1,128,2048]{2,1,0:T(8,128)}, f32[1,128]{1,0:T(1,128)}) custom-call(f32[1,128,2048]{2,1,0:T(8,128)} %sol_hbm.1, f32[1,128,2048]{2,1,0:T(8,128)} %dir_hbm.3, f32[2,128,1024]{2,1,0:T(8,128)} %get-tuple-element.11.nr_hbm, f32[2,128,1024]{2,1,0:T(8,128)} %get-tuple-element.12.prec_hbm, ...), custom_call_target="tpu_custom_call" | custom-call | tf_op jit(solution)/shard_map/finish/pallas_call | solution.py:655

commit v4 on v3

v4 whole, which is shorter than its diff:
```python
import functools

import jax
import jax.numpy as jnp
from jax import lax
from jax.experimental import pallas as pl
from jax.experimental.pallas import tpu as pltpu
from jax.sharding import PartitionSpec as P

F32 = jnp.float32
BF16 = jnp.bfloat16
MESH = pl.DeviceIdType.MESH

N_SUB = 32
N_GRP = 4
ROW = 8
N_X = N_SUB // ROW
W = 128
FB = 8
FACE = FB * W
REACH = 2


def split(x):
    hi = x.astype(BF16)
    lo = (x - hi.astype(F32)).astype(BF16)
    return hi, lo


def wide(x):
    return jnp.concatenate(split(x), 1)


def mm(x, w):
    return lax.dot_general(x, w, (((1,), (0,)), ((), ())), preferred_element_type=F32)


def mmt(x, w):
    return lax.dot_general(x, w, (((1,), (1,)), ((), ())), preferred_element_type=F32)


def mm3(x, w):
    xh, xl = split(x)
    wh, wl = split(w)
    return mm(jnp.concatenate([xh, xl], 1), jnp.concatenate([wh, wh], 0)) + mm(xh, wl)


def cols(b):
    return pl.ds(b * W, W)


def kernel(
    res_hbm, dir_hbm, rp_ref, slots, coup_hbm, diri_hbm, face_hbm, neum_hbm, pblk_ref, basis_hbm, cmat_hbm,
    cinv_hbm, patt,
    nr_hbm, prec_hbm, rows_ref,
    coup0, coup1, coup2, diri0, diri1, diri2, face, neum, basis, cmat, cinv, res,
    uf, uhl, yy, tt, ss, c2, nr, prec, nst, nf, bms, bmr, masks, crs, crr, cis, cir, ownc, steps, win, cors, corr_in,
    avec, z2, ar_p, ar_z,
    lsem, osem, dsend, drecv, nsend, nrecv, bsend, brecv, crsend, crrecv, cisend, cirecv, c2send, c2recv,
    wysend, wyrecv, wssend, wrecv, cosend, corecv, psend, precv, zsend, zrecv,
):
    i = lax.axis_index("sub")
    g = lax.axis_index("grp")
    row = i // ROW
    col = i % ROW

    def at_sub(k):
        return lax.rem(i + k + N_SUB, N_SUB)

    def at_grp(k):
        return lax.rem(g + k + N_GRP, N_GRP)

    def dev(s, t):
        return {"sub": s, "grp": t}

    neighbor = [dev(at_sub(-1), g), dev(at_sub(1), g), dev(i, at_grp(-1)), dev(i, at_grp(1))]
    y_peers = [dev(i, at_grp(k)) for k in range(1, N_GRP)]
    z_peers = [dev(row * ROW + lax.rem(col + k, ROW), g) for k in range(1, ROW)]
    plane = row * N_GRP + g
    many_plane = N_X * N_GRP

    def in_plane(k):
        other = lax.rem(plane + k, many_plane)
        return dev(other // N_GRP * ROW + col, lax.rem(other, N_GRP))

    p_peers = [in_plane(k) for k in range(1, many_plane)]
    reach = [k for k in range(-REACH, REACH + 1) if k != 0]
    s_peers = [dev(at_sub(k), g) for k in reach]
    odd = lax.rem(i, 2)
    far = [dev(at_sub(REACH), g), dev(at_sub(-REACH), g)]
    partner = dev(i + 1 - 2 * odd, g)

    local = []

    def load(src, dst):
        copy = pltpu.make_async_copy(src, dst, lsem.at[len(local)])
        copy.start()
        local.append(copy)
        return copy

    coup = (coup0, coup1, coup2)
    diri = (diri0, diri1, diri2)
    many = 4 * FB
    l_basis = load(basis_hbm.at[0], basis)
    l_dir = [load(dir_hbm.at[0, :, pl.ds(f * FACE, FACE)], uf.at[2 * f + 1]) for f in (1, 0)]
    l_face = load(face_hbm.at[0], face)
    l_interior = []
    for q in range(3):
        if q == 1:
            l_neum = load(neum_hbm.at[0], neum)
        l_interior.append(
            (
                load(coup_hbm.at[0, pl.ds(q * many, many)], coup[q]),
                load(diri_hbm.at[0, pl.ds(q * many, many)], diri[q]),
            )
        )
    l_res = [load(res_hbm.at[0, :, pl.ds(f * FACE, FACE)], res.at[f]) for f in range(2)]
    l_cinv = load(cinv_hbm.at[0], cinv)
    l_cmat = load(cmat_hbm.at[0], cmat)

    barrier = pltpu.get_barrier_semaphore()
    everyone = p_peers + z_peers + s_peers
    for peer in everyone:
        pl.semaphore_signal(barrier, inc=1, device_id=peer, device_id_type=MESH)
    pl.semaphore_wait(barrier, len(everyone))

    sent = []

    def send(src, dst, send_sem, recv_sem, peer):
        copy = pltpu.make_async_remote_copy(
            src_ref=src, dst_ref=dst, send_sem=send_sem, recv_sem=recv_sem, device_id=peer, device_id_type=MESH
        )
        copy.start()
        sent.append(copy)

    def arrived(ref, send_sem, recv_sem):
        pltpu.make_async_remote_copy(
            src_ref=ref, dst_ref=ref, send_sem=send_sem, recv_sem=recv_sem, device_id=neighbor[0], device_id_type=MESH
        ).wait_recv()

    chunks = ((0, 4), (4, 6), (6, FB))

    def chunk(h):
        return pl.ds(chunks[h][0] * W, (chunks[h][1] - chunks[h][0]) * W)

    for h, (start, stop) in enumerate(chunks):
        send(
            dir_hbm.at[0, :, pl.ds(FACE + start * W, (stop - start) * W)], uf.at[2, :, chunk(h)],
            dsend.at[h], drecv.at[h], neighbor[3],
        )
    send(dir_hbm.at[0, :, pl.ds(0, FACE)], uf.at[0], dsend.at[3], drecv.at[3], neighbor[1])

    l_basis.wait()
    pb_row = pblk_ref[...].astype(F32)
    basis_t = jnp.transpose(basis[...].astype(F32))
    for d in range(4):
        bms[d, 0:W, :] = basis_t
        bms[d, W : W + 8, :] = jnp.broadcast_to(pb_row - (slots[0, d] * FB).astype(F32), (8, W))

    def send_basis(d):
        send(bms.at[d], bmr.at[d ^ 1], bsend.at[d], brecv.at[d ^ 1], neighbor[d])

    def basis_arrived(d):
        arrived(bmr.at[d], bsend.at[d], brecv.at[d])
        nb_masks(d)

    for d in (2, 0, 3, 1):
        send_basis(d)
    def own_masks(d, carry):
        for b in range(FB):
            number = (slots[0, d] * FB + b).astype(F32)
            masks[d, b, :, 0:W] = jnp.where(pb_row == number, bms[0, 0:W, :], 0.0).astype(BF16)
        return carry

    lax.fori_loop(0, 4, own_masks, 0)

    def nb_masks(d):
        rel = bmr[d, W : W + 1, :]
        for b in range(FB):
            masks[d, b, :, W : 2 * W] = jnp.where(rel == float(b), bmr[d, 0:W, :], 0.0).astype(BF16)

    def coarse_pair(read, d):
        sums = [None, None]
        for b in range(FB):
            both = masks[d, b]
            part = mm(wide(read(b)), jnp.concatenate([both, both], 0))
            sums[b % 2] = part if sums[b % 2] is None else sums[b % 2] + part
        return sums[0] + sums[1]

    l_dir[0].wait()
    l_face.wait()
    for copy in l_interior[0]:
        copy.wait()

    def chain(jobs):
        first = []
        for (hi, lo), n in jobs:
            m = coup[n[0]][n[1]]
            first.append(wide(mm(jnp.concatenate([hi, lo], 1), jnp.concatenate([m, m], 0))))
        second = []
        for x, (_, n) in zip(first, jobs):
            m = diri[n[0]][n[1]]
            second.append(wide(mm(x, jnp.concatenate([m, m], 0))))
        third = []
        for x, (_, n) in zip(second, jobs):
            m = diri[n[0]][n[1]]
            third.append(wide(mmt(x, jnp.concatenate([m, m], 1))))
        out = []
        for x, (_, n) in zip(third, jobs):
            m = coup[n[0]][n[1]]
            out.append(mmt(x, jnp.concatenate([m, m], 1)))
        return out

    def interior(jobs, size=9):
        out = []
        for k in range(0, len(jobs), size):
            out += chain(jobs[k : k + size])
        return out

    def pair_of(d, b, e, c):
        hi = jnp.concatenate([uhl[d, 0:W, cols(b)], uhl[e, 0:W, cols(c)]], 1)
        lo = jnp.concatenate([uhl[d, W : 2 * W, cols(b)], uhl[e, W : 2 * W, cols(c)]], 1)
        return hi, lo

    def face_term(d, blocks):
        base = slots[0, d] * FB
        for b in blocks:
            hi, lo = split(uf[d, :, cols(b)])
            uhl[d, 0:W, cols(b)] = hi
            uhl[d, W : 2 * W, cols(b)] = lo
            m = face[base + b]
            yy[d, :, cols(b)] = mm(jnp.concatenate([hi, lo], 1), jnp.concatenate([m, m], 0))

    def within_jobs(d, pairs):
        base = slots[0, d] * FB
        return [(pair_of(d, b, d, b + q + 1), (q, base + b)) for q, b in pairs]

    def within_sink(d, pairs, outs):
        for (q, b), out in zip(pairs, outs):
            yy[d, :, cols(b)] += out[:, :W]
            yy[d, :, cols(b + q + 1)] += out[:, W:]

    def within(d, pairs):
        within_sink(d, pairs, interior(within_jobs(d, pairs)))

    inside = [(q, b) for q in range(3) for b in range(FB - 1 - q)]
    early, middle, late = [[(q, b) for q, b in inside if start <= b + q + 1 < stop] for start, stop in chunks]
    across = [(q, b) for q in range(3) for b in range(FB - 1 - q, FB)]

    def direction_of(slot):
        where = jnp.int32(0)
        for d in range(1, 4):
            where = jnp.where(slots[0, d] == slot, jnp.int32(d), where)
        return where

    def straddling_jobs(places):
        jobs = []
        for p in places:
            slot = lax.rem(slots[0, 2] + 1 + p, 4)
            this = direction_of(slot)
            after = direction_of(lax.rem(slot + 1, 4))
            for q, b in across:
                jobs.append((pair_of(this, b, after, b + q + 1 - FB), (q, slot * FB + b)))
        return jobs

    def straddling_sink(places, outs):
        sinks = [(p, b - FB + 3, b + q + 1 - FB) for p in places for q, b in across]
        heads, tails = {}, {}
        for (p, h, m), out in zip(sinks, outs):
            heads[p, h] = heads[p, h] + out[:, :W] if (p, h) in heads else out[:, :W]
            tails[p, m] = tails[p, m] + out[:, W:] if (p, m) in tails else out[:, W:]
        for (p, m), value in heads.items():
            tt[p, :, cols(m)] = value
        for (p, m), value in tails.items():
            ss[p, :, cols(m)] = value

    def return_piece(f, k):
        piece = cols(k)
        send(
            yy.at[2 * f, :, piece], c2.at[f, :, piece], c2send.at[f, k], c2recv.at[f, k], neighbor[2 * f]
        )

    def returned(f, blocks):
        for k in blocks:
            piece = cols(k)
            arrived(c2.at[f, :, piece], c2send.at[f, k], c2recv.at[f, k])

    def first_step(v, value):
        ownc[v] = value
        steps[v, g] = mm3(value, cinv[...])
        for k, peer in enumerate(y_peers):
            send(steps.at[v, g], steps.at[v, g], wysend.at[v, k], wyrecv.at[v, g], peer)

    def forward(k):
        piece = at_grp(k)
        if k > 0:
            for v in range(2):
                arrived(steps.at[v, piece], wysend.at[v, 0], wyrecv.at[v, piece])
        win[REACH, piece] = 0.5 * (steps[0, piece] - avec[...] * steps[1, piece])
        for n, (place, peer) in enumerate(zip((0, 2 * REACH, 1 + 2 * odd), far + [partner])):
            send(win.at[REACH, piece], win.at[place, piece], wssend.at[k, n], wrecv.at[place, piece], peer)

    def relay(k):
        piece = at_grp(k)
        place, there = 2 * REACH * (1 - odd), 3 - 2 * odd
        arrived(win.at[place, piece], wssend.at[0, 0], wrecv.at[place, piece])
        send(win.at[place, piece], win.at[there, piece], wssend.at[k, 3], wrecv.at[there, piece], partner)

    def complete():
        for k in range(N_GRP):
            piece = at_grp(k)
            for place in (2 * REACH * odd, 1, 3):
                arrived(win.at[place, piece], wssend.at[0, 0], wrecv.at[place, piece])

    face_term(3, range(FB))
    within(3, [(q, b) for q, b in inside if q == 0])
    for copy in l_interior[1]:
        copy.wait()
    within(3, [(q, b) for q, b in inside if q == 1])
    for copy in l_interior[2]:
        copy.wait()
    within(3, [(q, b) for q, b in inside if q == 2])
    l_neum.wait()
    for f in (1, 0):
        start = slots[0, 2 * f] * FB

        def to_f32(b, carry, f=f, start=start):
            nst[f, b] = neum[start + b].astype(F32)
            return carry

        lax.fori_loop(0, FB, to_f32, 0)
        send(nst.at[f], nf.at[f], nsend.at[f], nrecv.at[f], neighbor[2 * f])

    basis_arrived(3)
    basis_arrived(1)
    for copy in l_res:
        copy.wait()

    pairs = [coarse_pair(lambda b, f=f: res[f, :, cols(b)], 2 * f + 1) for f in range(2)]
    ownc[0] = pairs[0][:, :W] + pairs[1][:, :W]
    for f in range(2):
        crs[f] = pairs[f][:, W:]
    for f in range(2):
        send(crs.at[f], crr.at[f], crsend.at[f], crrecv.at[f], neighbor[2 * f + 1])

    l_dir[1].wait()
    face_term(1, range(FB))
    within(1, inside)

    arrived(uf.at[2, :, chunk(0)], dsend.at[0], drecv.at[0])
    face_term(2, range(*chunks[0]))
    within(2, early)
    arrived(uf.at[0], dsend.at[3], drecv.at[3])
    face_term(0, range(FB))
    within(0, inside)
    straddling_sink((0, 1, 2), interior(straddling_jobs((0, 1, 2))))
    place = lax.rem(slots[0, 0] - slots[0, 2] + 7, 4)
    for m in range(3):
        yy[0, :, cols(FB - 3 + m)] += tt[place, :, cols(m)]
    for k in range(3, FB):
        return_piece(0, k)
    basis_arrived(0)
    arrived(uf.at[2, :, chunk(1)], dsend.at[1], drecv.at[1])
    face_term(2, range(*chunks[1]))
    within(2, middle)
    for m in range(3):
        yy[2, :, cols(m)] += ss[2, :, cols(m)]
    return_piece(1, 0)
    return_piece(1, 1)
    arrived(uf.at[2, :, chunk(2)], dsend.at[2], drecv.at[2])
    face_term(2, range(*chunks[2]))
    outs = interior(within_jobs(2, late) + straddling_jobs((3,)), 6)
    within_sink(2, late, outs[: len(late)])
    straddling_sink((3,), outs[len(late) :])
    for d in range(4):
        place = lax.rem(slots[0, d] - slots[0, 2] + 7, 4)
        before = lax.rem(slots[0, d] - slots[0, 2] + 6, 4)
        for m in range(3):
            if d != 2:
                yy[d, :, cols(m)] += ss[before, :, cols(m)]
            if d != 0:
                yy[d, :, cols(FB - 3 + m)] += tt[place, :, cols(m)]

    def folded(x):
        return jnp.sum(jnp.transpose(x).reshape(W // 8, 8, W), axis=0)

    stages = (
        (ar_p, psend, precv, many_plane, plane, p_peers),
        (ar_z, zsend, zrecv, ROW, col, z_peers),
    )

    def stage_send(which, stage, value):
        buf, ssem, rsem, count, me, peers = stages[stage]
        buf[which, me] = value
        for k, peer in enumerate(peers):
            send(buf.at[which, me], buf.at[which, me], ssem.at[which, k], rsem.at[which, me], peer)

    def stage_wait(which, stage):
        buf, ssem, rsem, count, me, peers = stages[stage]
        for k in range(1, count):
            other = lax.rem(me + k, count)
            arrived(buf.at[which, other], ssem.at[which, 0], rsem.at[which, other])
        total = buf[which, 0]
        for k in range(1, count):
            total = total + buf[which, k]
        return total

    def curve(d, acc):
        for b in range(FB):
            acc = acc + uf[d, :, cols(b)] * yy[d, :, cols(b)]
        return acc

    stage_send(0, 0, folded(lax.fori_loop(0, 4, curve, jnp.zeros((W, W), F32))))

    basis_arrived(2)

    for first in (2, 0):
        pairs = [coarse_pair(lambda b, d=d: yy[d, :, cols(b)], d) for d in (first, first + 1)]
        for d, pair in zip((first, first + 1), pairs):
            cis[d] = pair[:, W:]
            send(cis.at[d], cir.at[d ^ 1], cisend.at[d], cirecv.at[d ^ 1], neighbor[d])
        both = pairs[0][:, :W] + pairs[1][:, :W]
        ownc[1] = both if first == 2 else ownc[1] + both

    for f in range(2):
        arrived(crr.at[f], crsend.at[f], crrecv.at[f])
    l_cinv.wait()
    first_step(0, ownc[0] + (crr[0] + crr[1]))
    stage_send(0, 1, stage_wait(0, 0))
    for k in range(3):
        return_piece(0, k)
    for k in range(2, 3):
        return_piece(1, k)
    for d in range(4):
        arrived(cir.at[d], cisend.at[d], cirecv.at[d])
    first_step(1, ownc[1] + ((cir[0] + cir[1]) + (cir[2] + cir[3])))
    for k in range(3, FB):
        return_piece(1, k)
    rp_row = rp_ref[...]
    curvature = jnp.sum(stage_wait(0, 1), axis=0, keepdims=True)
    step_row = rp_row / curvature
    avec[...] = jnp.transpose(jnp.broadcast_to(step_row, (W, W)))
    forward(0)
    for k in range(1, N_GRP):
        forward(k)
    relay(0)

    outs = []

    def store(src, dst):
        copy = pltpu.make_async_copy(src, dst, osem.at[len(outs)])
        copy.start()
        outs.append(copy)

    z2[...] = jnp.zeros_like(z2)

    def own_face(f, blocks):
        a = avec[...]
        base = slots[0, 2 * f + 1] * FB
        acc = z2[...]
        for b in blocks:
            new = res[f, :, cols(b)] - a * (yy[2 * f + 1, :, cols(b)] + c2[f, :, cols(b)])
            nr[f, :, cols(b)] = new
            mine = neum[base + b]
            theirs = nf[f, b].astype(BF16)
            both = jnp.concatenate([mine, theirs], 1)
            z = mm(wide(0.5 * new), jnp.concatenate([both, both], 0))
            acc = acc + (z[:, :W] * z[:, :W] + z[:, W:] * z[:, W:])
            lhs = jnp.concatenate([wide(z[:, :W]), wide(z[:, W:])], 1)
            prec[f, :, cols(b)] = mmt(lhs, jnp.concatenate([mine, mine, theirs, theirs], 1))
        z2[...] = acc

    returned(0, range(FB))
    arrived(nf.at[0], nsend.at[0], nrecv.at[0])
    own_face(0, range(FB))
    relay(1)
    arrived(nf.at[1], nsend.at[1], nrecv.at[1])
    returned(1, range(4))
    own_face(1, range(4))
    relay(2)
    returned(1, range(4, FB))
    own_face(1, range(4, FB))
    for f in range(2):
        store(nr.at[f], nr_hbm.at[f])

    relay(3)
    complete()
    l_cmat.wait()
    adjacent = None
    for k in range(9):
        entry = patt[0, k]
        place = jnp.minimum(lax.rem(entry // N_GRP - i + REACH + N_SUB, N_SUB), 2 * REACH)
        part = mm3(win[place, lax.rem(entry, N_GRP)], cmat[k])
        adjacent = part if adjacent is None else adjacent + part
    coarse_res = 0.5 * (ownc[0] - avec[...] * ownc[1])
    corr = win[REACH, g] + mm3(coarse_res - adjacent, cinv[...])
    cors[...] = corr
    stage_send(1, 0, folded(z2[...] + corr * coarse_res))
    for f in (1, 0):
        send(cors, corr_in.at[f], cosend.at[f], corecv.at[f], neighbor[2 * f])
    stage_send(1, 1, stage_wait(1, 0))
    for f in range(2):
        arrived(corr_in.at[f], cosend.at[f], corecv.at[f])

    def spread_back(f, carry):
        lhs = jnp.concatenate([wide(cors[...]), wide(corr_in[f])], 1)
        for b in range(FB):
            own = masks[2 * f + 1, b, :, 0:W]
            other = masks[2 * f + 1, b, :, W : 2 * W]
            back = mmt(lhs, jnp.concatenate([own, own, other, other], 1))
            prec[f, :, cols(b)] = 0.5 * (prec[f, :, cols(b)] + back)
        return carry

    lax.fori_loop(0, 2, spread_back, 0)
    for f in range(2):
        store(prec.at[f], prec_hbm.at[f])

    product = jnp.sum(stage_wait(1, 1), axis=0, keepdims=True)
    rows_ref[0:1, :] = step_row
    rows_ref[1:2, :] = product / rp_row
    rows_ref[2:3, :] = product
    for copy in sent:
        copy.wait_send()
    for copy in outs:
        copy.wait()


def finish(
    sol_hbm, dir_hbm, nr_hbm, prec_hbm, rows, nsol_hbm, nres_hbm, ndir_hbm, nprod_ref, sol, dirn, nr, prec, lsem, osem
):
    def face(ref, f):
        return ref.at[0, :, pl.ds(f * FACE, FACE)]

    loads = [
        [
            pltpu.make_async_copy(src, dst, lsem.at[f, k])
            for k, (src, dst) in enumerate(
                (
                    (nr_hbm.at[f], nr.at[f]),
                    (face(sol_hbm, f), sol.at[f]),
                    (face(dir_hbm, f), dirn.at[f]),
                    (prec_hbm.at[f], prec.at[f]),
                )
            )
        ]
        for f in range(2)
    ]
    for copy in loads[0] + loads[1]:
        copy.start()
    step = jnp.transpose(jnp.broadcast_to(rows[0:1, :], (W, W)))
    ratio = jnp.transpose(jnp.broadcast_to(rows[1:2, :], (W, W)))
    nprod_ref[...] = rows[2:3, :]
    outs = []

    def store(src, dst):
        copy = pltpu.make_async_copy(src, dst, osem.at[len(outs)])
        copy.start()
        outs.append(copy)

    for f in range(2):
        loads[f][0].wait()
        store(nr.at[f], face(nres_hbm, f))
        loads[f][1].wait()
        loads[f][2].wait()
        for b in range(FB):
            sol[f, :, cols(b)] += step * dirn[f, :, cols(b)]
        store(sol.at[f], face(nsol_hbm, f))
        loads[f][3].wait()
        for b in range(FB):
            prec[f, :, cols(b)] += ratio * dirn[f, :, cols(b)]
        store(prec.at[f], face(ndir_hbm, f))
    for copy in outs:
        copy.wait()


def shards(
    solution,
    residual,
    direction,
    residual_product,
    neighbor_slots,
    coupling,
    dirichlet_factor,
    face_block,
    neumann_factor,
    primal_block,
    primal_basis,
    coarse_matrix,
    coarse_block_inverse,
    coarse_pattern,
):
    hbm = pl.BlockSpec(memory_space=pl.ANY)
    vmem = pl.BlockSpec(memory_space=pltpu.VMEM)
    smem = pl.BlockSpec(memory_space=pltpu.SMEM)
    dma = pltpu.SemaphoreType.DMA
    big = jax.ShapeDtypeStruct((1, W, 2 * FACE), F32)
    pair = jax.ShapeDtypeStruct((2, W, FACE), F32)
    nr, prec, rows = pl.pallas_call(
        kernel,
        out_shape=(pair, pair, jax.ShapeDtypeStruct((8, W), F32)),
        in_specs=[hbm, hbm, vmem, smem, hbm, hbm, hbm, hbm, vmem, hbm, hbm, hbm, smem],
        out_specs=(hbm, hbm, vmem),
        scratch_shapes=[
            *[pltpu.VMEM((32, 2 * W, W), BF16)] * 3,
            *[pltpu.VMEM((32, W, W), BF16)] * 3,
            pltpu.VMEM((32, W, W), BF16),
            pltpu.VMEM((32, W, W), BF16),
            pltpu.VMEM((W, W), BF16),
            pltpu.VMEM((9, W, W), F32),
            pltpu.VMEM((W, W), F32),
            pltpu.VMEM((2, W, FACE), F32),
            pltpu.VMEM((4, W, FACE), F32),
            pltpu.VMEM((4, 2 * W, FACE), BF16),
            pltpu.VMEM((4, W, FACE), F32),
            pltpu.VMEM((4, W, 3 * W), F32),
            pltpu.VMEM((4, W, 3 * W), F32),
            pltpu.VMEM((2, W, FACE), F32),
            pltpu.VMEM((2, W, FACE), F32),
            pltpu.VMEM((2, W, FACE), F32),
            pltpu.VMEM((2, FB, W, W), F32),
            pltpu.VMEM((2, FB, W, W), F32),
            pltpu.VMEM((4, W + 8, W), F32),
            pltpu.VMEM((4, W + 8, W), F32),
            pltpu.VMEM((4, FB, W, 2 * W), BF16),
            pltpu.VMEM((2, W, W), F32),
            pltpu.VMEM((2, W, W), F32),
            pltpu.VMEM((4, W, W), F32),
            pltpu.VMEM((4, W, W), F32),
            pltpu.VMEM((2, W, W), F32),
            pltpu.VMEM((2, N_GRP, W, W), F32),
            pltpu.VMEM((2 * REACH + 1, N_GRP, W, W), F32),
            pltpu.VMEM((W, W), F32),
            pltpu.VMEM((2, W, W), F32),
            pltpu.VMEM((W, W), F32),
            pltpu.VMEM((W, W), F32),
            pltpu.VMEM((2, N_X * N_GRP, 8, W), F32),
            pltpu.VMEM((2, ROW, 8, W), F32),
            dma((15,)),
            dma((4,)),
            dma((4,)), dma((4,)),
            dma((2,)), dma((2,)),
            dma((4,)), dma((4,)),
            dma((2,)), dma((2,)),
            dma((4,)), dma((4,)),
            dma((2, FB)), dma((2, FB)),
            dma((2, 3)), dma((2, N_GRP)), dma((N_GRP, 4)), dma((2 * REACH + 1, N_GRP)),
            dma((2,)), dma((2,)),
            dma((2, N_X * N_GRP)), dma((2, N_X * N_GRP)),
            dma((2, ROW)), dma((2, ROW)),
        ],
        compiler_params=pltpu.CompilerParams(
            collective_id=0, has_side_effects=True, vmem_limit_bytes=60 * 1024 * 1024
        ),
        name="pcg_step",
    )(
        residual,
        direction,
        residual_product.reshape(1, W),
        neighbor_slots,
        coupling,
        dirichlet_factor,
        face_block,
        neumann_factor,
        primal_block,
        primal_basis,
        coarse_matrix,
        coarse_block_inverse,
        coarse_pattern,
    )
    nsol, nres, ndir, nprod = pl.pallas_call(
        finish,
        out_shape=(big, big, big, jax.ShapeDtypeStruct((1, W), F32)),
        in_specs=[hbm, hbm, hbm, hbm, vmem],
        out_specs=(hbm, hbm, hbm, vmem),
        scratch_shapes=[
            pltpu.VMEM((2, W, FACE), F32),
            pltpu.VMEM((2, W, FACE), F32),
            pltpu.VMEM((2, W, FACE), F32),
            pltpu.VMEM((2, W, FACE), F32),
            dma((2, 4)),
            dma((6,)),
        ],
        name="finish",
    )(solution, direction, nr, prec, rows)
    return nsol, nres, ndir, nprod.reshape(W)


def solution(mesh):
    both = ("sub", "grp")

    def split_first(rank):
        return P(both, *([None] * (rank - 1)))

    return jax.shard_map(
        shards,
        mesh=mesh,
        in_specs=(
            split_first(3), split_first(3), split_first(3), P(), split_first(2), split_first(4), split_first(4),
            split_first(4), split_first(4), split_first(2), split_first(3), split_first(4), split_first(3),
            split_first(2),
        ),
        out_specs=(split_first(3), split_first(3), split_first(3), P()),
        check_vma=False,
    )
```

time: 66.6 us -> 63.9 us (0.959); the launches traced: 66.1 us -> 62.7 us
  Pallas kernels: 65.3 us -> 61.9 us
    pallas_call x1, Pallas kernels: 60.8 us -> 57.4 us  [shards(): pl.pallas_call(kernel, out_shape=(pair, pair, jax.ShapeDtypeStruct((8, W)...]
where the time goes in v4:
time: 63.9 us; the launch traced here: 62.7 us
  Pallas kernels  61.9 us (97%)
  between operations  0.82 us (1%)
    pallas_call x1, Pallas kernels, shards(): pl.pallas_call(kernel, out_shape=(pair, pair, jax.ShapeDtypeStruct((8, W)...  57.4 us
    pallas_call x1, Pallas kernels, shards(): pl.pallas_call(finish, out_shape=(big, big, big, jax.ShapeDtypeStruct((1,...  4.52 us

profile of v4, /device:TPU:0, one launch (start us, length us, event | category | flops | bytes accessed | tf_op | source)
XLA Modules:
  0.0 62.7 jit_solution(3858938935191133508)
XLA Ops:
  0.6 57.4 %pcg_step.1 = (f32[2,128,1024]{2,1,0:T(8,128)}, f32[2,128,1024]{2,1,0:T(8,128)}, f32[8,128]{1,0:T(8,128)}) custom-call(f32[1,128,2048]{2,1,0:T(8,128)} %res_hbm.1, f32[1,128,2048]{2,1,0:T(8,128)} %dir_hbm.3, f32[1,128]{1,0:T(1,128)} %bitcast.2, s32[1,4]{1,0:T(1,128)} %slots.1, bf16[1,96,256,128]{3,2,1,0:T(8,128)(2,1)} %coup_hbm.1, ...), custom_call_target="tpu_custom_call" | custom-call | tf_op jit(solution)/shard_map/pcg_step/pallas_call | solution.py:598
  58.0 4.5 %finish.1 = (f32[1,128,2048]{2,1,0:T(8,128)}, f32[1,128,2048]{2,1,0:T(8,128)}, f32[1,128,2048]{2,1,0:T(8,128)}, f32[1,128]{1,0:T(1,128)}) custom-call(f32[1,128,2048]{2,1,0:T(8,128)} %sol_hbm.1, f32[1,128,2048]{2,1,0:T(8,128)} %dir_hbm.3, f32[2,128,1024]{2,1,0:T(8,128)} %get-tuple-element.11.nr_hbm, f32[2,128,1024]{2,1,0:T(8,128)} %get-tuple-element.12.prec_hbm, ...), custom_call_target="tpu_custom_call" | custom-call | tf_op jit(solution)/shard_map/finish/pallas_call | solution.py:670

commit v5 on v4

--- a/solution.py
+++ b/solution.py
@@ -148,7 +148,10 @@
             dir_hbm.at[0, :, pl.ds(FACE + start * W, (stop - start) * W)], uf.at[2, :, chunk(h)],
             dsend.at[h], drecv.at[h], neighbor[3],
         )
-    send(dir_hbm.at[0, :, pl.ds(0, FACE)], uf.at[0], dsend.at[3], drecv.at[3], neighbor[1])
+    half = FACE // 2
+    for h in range(2):
+        part = pl.ds(h * half, half)
+        send(dir_hbm.at[0, :, part], uf.at[0, :, part], dsend.at[3 + h], drecv.at[3 + h], neighbor[1])
 
     l_basis.wait()
     pb_row = pblk_ref[...].astype(F32)
@@ -164,7 +167,7 @@
         arrived(bmr.at[d], bsend.at[d], brecv.at[d])
         nb_masks(d)
 
-    for d in (2, 0, 3, 1):
+    for d in (2, 0):
         send_basis(d)
     def own_masks(d, carry):
         for b in range(FB):
@@ -342,17 +345,22 @@
         crs[f] = pairs[f][:, W:]
     for f in range(2):
         send(crs.at[f], crr.at[f], crsend.at[f], crrecv.at[f], neighbor[2 * f + 1])
+    send_basis(3)
+    send_basis(1)
 
     l_dir[1].wait()
     face_term(1, range(FB))
     within(1, inside)
 
+    arrived(uf.at[0, :, pl.ds(0, half)], dsend.at[3], drecv.at[3])
+    face_term(0, range(FB // 2))
+    within(0, early)
     arrived(uf.at[2, :, chunk(0)], dsend.at[0], drecv.at[0])
     face_term(2, range(*chunks[0]))
     within(2, early)
-    arrived(uf.at[0], dsend.at[3], drecv.at[3])
-    face_term(0, range(FB))
-    within(0, inside)
+    arrived(uf.at[0, :, pl.ds(half, half)], dsend.at[4], drecv.at[4])
+    face_term(0, range(FB // 2, FB))
+    within(0, middle + late)
     straddling_sink((0, 1, 2), interior(straddling_jobs((0, 1, 2))))
     place = lax.rem(slots[0, 0] - slots[0, 2] + 7, 4)
     for m in range(3):
@@ -637,7 +645,7 @@
             pltpu.VMEM((2, ROW, 8, W), F32),
             dma((15,)),
             dma((4,)),
-            dma((4,)), dma((4,)),
+            dma((5,)), dma((5,)),
             dma((2,)), dma((2,)),
             dma((4,)), dma((4,)),
             dma((2,)), dma((2,)),

time: 63.9 us -> 62.8 us (0.983)
  Pallas kernels: 61.9 us -> 60.8 us
    pallas_call x1, Pallas kernels: 57.4 us -> 56.3 us  [shards(): pl.pallas_call(kernel, out_shape=(pair, pair, jax.ShapeDtypeStruct((8, W)...]
where the time goes in v5:
time: 62.8 us; the launch traced here: 61.7 us
  Pallas kernels  60.8 us (97%)
  between operations  0.82 us (1%)
    pallas_call x1, Pallas kernels, shards(): pl.pallas_call(kernel, out_shape=(pair, pair, jax.ShapeDtypeStruct((8, W)...  56.3 us
    pallas_call x1, Pallas kernels, shards(): pl.pallas_call(finish, out_shape=(big, big, big, jax.ShapeDtypeStruct((1,...  4.52 us

profile of v5, /device:TPU:0, one launch (start us, length us, event | category | flops | bytes accessed | tf_op | source)
XLA Modules:
  0.0 61.7 jit_solution(9955567634485614954)
XLA Ops:
  0.6 56.3 %pcg_step.1 = (f32[2,128,1024]{2,1,0:T(8,128)}, f32[2,128,1024]{2,1,0:T(8,128)}, f32[8,128]{1,0:T(8,128)}) custom-call(f32[1,128,2048]{2,1,0:T(8,128)} %res_hbm.1, f32[1,128,2048]{2,1,0:T(8,128)} %dir_hbm.3, f32[1,128]{1,0:T(1,128)} %bitcast.2, s32[1,4]{1,0:T(1,128)} %slots.1, bf16[1,96,256,128]{3,2,1,0:T(8,128)(2,1)} %coup_hbm.1, ...), custom_call_target="tpu_custom_call" | custom-call | tf_op jit(solution)/shard_map/pcg_step/pallas_call | solution.py:606
  57.0 4.5 %finish.1 = (f32[1,128,2048]{2,1,0:T(8,128)}, f32[1,128,2048]{2,1,0:T(8,128)}, f32[1,128,2048]{2,1,0:T(8,128)}, f32[1,128]{1,0:T(1,128)}) custom-call(f32[1,128,2048]{2,1,0:T(8,128)} %sol_hbm.1, f32[1,128,2048]{2,1,0:T(8,128)} %dir_hbm.3, f32[2,128,1024]{2,1,0:T(8,128)} %get-tuple-element.11.nr_hbm, f32[2,128,1024]{2,1,0:T(8,128)} %get-tuple-element.12.prec_hbm, ...), custom_call_target="tpu_custom_call" | custom-call | tf_op jit(solution)/shard_map/finish/pallas_call | solution.py:678
